TPU v7x, 128 devices: a whole 4x4x4 slice. The times are simulated.
128 devices in a mesh: ty: 8 (over x, core), tx: 16 (over y, z).
Axes of the slice: x: 4, y: 4, z: 4, core: 2. Of those that a mesh axis runs over, the one named last changes fastest.
Arguments:
- measured: float32 [8, 16, 32, 128, 128], P('ty', 'tx'), may hold values from 0 to 4
- positions: int32 [8, 16, 32, 2], P('ty', 'tx'), may hold values from 0 to 511, as said below
- owners: int32 [8, 16, 32], P('ty', 'tx'), may hold values from 0 to 127, as said below
- counts: int32 [8, 16], P('ty', 'tx'), may hold values from 16 to 32, as said below
- object_field: float32 [2, 4096, 8192], P(None, 'ty', 'tx'), may hold values from -4 to 4
- probe_field: float32 [2, 128, 128], replicated, may hold values from -6 to 6
Outputs:
- new_object: float32 [2, 4096, 8192], P(None, 'ty', 'tx')
- new_probe: float32 [2, 128, 128], replicated
Inputs may be any that keep to these rules, and one draw needn't show every extreme that they name: `positions`: for a live slot the entry is a cell of the owner's tile: row below 512, column below 512; other slots hold arbitrary cells of a tile. The owner of a live slot is the holding device's own tile or one of the up to eight tiles beside it (diagonals included). From one device at most 2 live slots go to any one other tile, and in every draw some tile receives exactly 2 from each of its eight neighbours. Slots that are not live hold arbitrary owners. `counts`: some device is full (32 live slots) in every draw.
All inputs are finite; a program needn't handle non-finite values.
Results may differ from a plain program's by a relative error of at most 0.0003.
Values sent between devices are 32-bit elements; how exact they have to be, the bound alone decides.
A program may use at most 128 MiB of HBM per device.

v0:
```python
import math

import jax
import jax.numpy as jnp
from jax import lax
from jax.sharding import PartitionSpec as P

M = 128
MOVE = 2
BLK = 8


offset_level = 1.0
floor_level = 1.0
tiny_level = 1e-06


def padded_2(value, sides, width):
    for axis, dim in sides:
        devices, length = (lax.axis_size(axis), value.shape[dim])
        up = [(i, (i + 1) % devices) for i in range(devices - 1)]
        down = [(j, i) for i, j in up]
        last = lax.slice_in_dim(value, length - width, length, axis=dim)
        leading = lax.slice_in_dim(value, 0, width, axis=dim)
        before = lax.ppermute(last, axis, up)
        after = lax.ppermute(leading, axis, down)
        value = jnp.concatenate([before, value, after], axis=dim)
    return value


def from_behind(block, axis, distance):
    devices = range(lax.axis_size(axis))
    route = [(i - distance, i) for i in devices if i - distance in devices]
    return lax.ppermute(block, axis, route)


def dft_tables(length_side):
    row_ids = lax.broadcasted_iota(jnp.int32, (length_side, length_side), 0)
    col_ids = lax.broadcasted_iota(jnp.int32, (length_side, length_side), 1)
    phase = (row_ids * col_ids % length_side).astype(jnp.float32) * (2.0 * math.pi / length_side)
    factor = 1.0 / math.sqrt(length_side)
    return (jnp.cos(phase) * factor, -jnp.sin(phase) * factor)


def transform(real_part, imag_part, cosine_table, sine_table):
    highest = lax.Precision.HIGHEST
    left_real = jnp.einsum("jk,bkl->bjl", cosine_table, real_part, precision=highest) - jnp.einsum(
        "jk,bkl->bjl", sine_table, imag_part, precision=highest
    )
    left_imag = jnp.einsum("jk,bkl->bjl", cosine_table, imag_part, precision=highest) + jnp.einsum(
        "jk,bkl->bjl", sine_table, real_part, precision=highest
    )
    outer_real = jnp.einsum("bjk,kl->bjl", left_real, cosine_table, precision=highest) - jnp.einsum(
        "bjk,kl->bjl", left_imag, sine_table, precision=highest
    )
    outer_imag = jnp.einsum("bjk,kl->bjl", left_real, sine_table, precision=highest) + jnp.einsum(
        "bjk,kl->bjl", left_imag, cosine_table, precision=highest
    )
    return (outer_real, outer_imag)


def pattern_terms(probe_field, patches, measured_block, live_mask, cosine_table, sine_table):
    probe_real = probe_field[0]
    probe_imag = probe_field[1]
    patch_real = patches[:, 0]
    patch_imag = patches[:, 1]
    exit_real = probe_real * patch_real - probe_imag * patch_imag
    exit_imag = probe_real * patch_imag + probe_imag * patch_real
    far_real, far_imag = transform(exit_real, exit_imag, cosine_table, sine_table)
    power = far_real * far_real + far_imag * far_imag
    ratio = 1.0 - measured_block / (power + offset_level)
    chi_real, chi_imag = transform(far_real * ratio, far_imag * ratio, cosine_table, -sine_table)
    chi_real = chi_real * live_mask[:, None, None]
    chi_imag = chi_imag * live_mask[:, None, None]
    object_real = probe_real * chi_real + probe_imag * chi_imag
    object_imag = probe_real * chi_imag - probe_imag * chi_real
    lighting = (probe_real * probe_real + probe_imag * probe_imag)[None] * live_mask[:, None, None]
    spread = jnp.stack([object_real, object_imag, lighting], axis=1)
    grad_real = jnp.sum(patch_real * chi_real + patch_imag * chi_imag, axis=0)
    grad_imag = jnp.sum(patch_real * chi_imag - patch_imag * chi_real, axis=0)
    weight = jnp.sum(
        (patch_real * patch_real + patch_imag * patch_imag) * live_mask[:, None, None], axis=0
    )
    return (spread, grad_real, grad_imag, weight)


def add_patches(accumulated, spread, start_rows, start_cols):
    zero_index = jnp.zeros((), jnp.int32)

    def add_one(patch_id, current):
        row_start = start_rows[patch_id]
        col_start = start_cols[patch_id]
        window = lax.dynamic_slice(current, (zero_index, row_start, col_start), spread.shape[1:])
        return lax.dynamic_update_slice(
            current, window + spread[patch_id], (zero_index, row_start, col_start)
        )

    return lax.fori_loop(0, spread.shape[0], add_one, accumulated)


def offsets(slot_tags, row_here, col_here, grid_cols):
    owner_id = slot_tags[:, 2] - 1
    is_valid = owner_id >= 0
    safe_owner = jnp.maximum(owner_id, 0)
    return (is_valid, safe_owner // grid_cols - row_here, safe_owner % grid_cols - col_here)


def select_slots(chosen, capacity, slot_rows, slot_tags):
    slot_count = chosen.shape[0]
    sort_key = jnp.where(chosen, 0, slot_count) + jnp.arange(slot_count, dtype=jnp.int32)
    picked = jnp.argsort(sort_key)[:capacity]
    kept_mask = jnp.take(chosen, picked)
    return (
        jnp.take(slot_rows, picked, axis=0),
        jnp.where(kept_mask[:, None], jnp.take(slot_tags, picked, axis=0), 0),
    )


def shards(measured, positions, owners, counts, object_field, probe_field):
    tile_rows = object_field.shape[1]
    tile_cols = object_field.shape[2]
    rim_width = M // 2
    grid_cols = lax.axis_size("tx")
    row_here = lax.axis_index("ty")
    col_here = lax.axis_index("tx")
    self_index = row_here * grid_cols + col_here
    padded = padded_2(object_field, (("ty", 1), ("tx", 2)), rim_width)
    own_rows = measured[0, 0]
    slot_ids = jnp.arange(own_rows.shape[0], dtype=jnp.int32)
    slot_alive = slot_ids < counts[0, 0]
    slot_info = jnp.concatenate([positions[0, 0], owners[0, 0][:, None]], axis=1) + 1
    own_tags = jnp.where(slot_alive[:, None], slot_info, 0)
    is_valid, row_offset, col_offset = offsets(own_tags, row_here, col_here, grid_cols)
    piece_rows = [own_rows]
    piece_tags = [own_tags]
    neighbours = [(-1, -1), (-1, 0), (-1, 1), (0, -1), (0, 1), (1, -1), (1, 0), (1, 1)]
    for down_step, right_step in neighbours:
        chosen = is_valid & (row_offset == down_step) & (col_offset == right_step)
        sent_rows, sent_tags = select_slots(chosen, MOVE, own_rows, own_tags)
        if down_step == 0:
            sent_rows, sent_tags = from_behind((sent_rows, sent_tags), "tx", right_step)
        elif right_step == 0:
            sent_rows, sent_tags = from_behind((sent_rows, sent_tags), "ty", down_step)
        else:
            sent_rows, sent_tags = from_behind((sent_rows, sent_tags), "tx", right_step)
            sent_rows, sent_tags = from_behind((sent_rows, sent_tags), "ty", down_step)
        piece_rows.append(sent_rows)
        piece_tags.append(sent_tags)
    all_rows = jnp.concatenate(piece_rows, axis=0)
    all_tags = jnp.concatenate(piece_tags, axis=0)
    valid_all = all_tags[:, 2] - 1 == self_index
    slot_total = all_rows.shape[0]
    slot_index = jnp.arange(slot_total, dtype=jnp.int32)
    slot_order = jnp.argsort(jnp.where(valid_all, 0, slot_total) + slot_index)
    block_turns = (jnp.sum(valid_all.astype(jnp.int32)) + BLK - 1) // BLK
    cosine_table, sine_table = dft_tables(M)
    zero_index = jnp.zeros((), jnp.int32)

    def one_block(block_id, state_carry):
        accumulated, grad_real, grad_imag, weight = state_carry
        picked = lax.dynamic_slice_in_dim(slot_order, block_id * BLK, BLK)
        block_rows = jnp.take(all_rows, picked, axis=0)
        block_tags = jnp.take(all_tags, picked, axis=0)
        live_mask = jnp.take(valid_all, picked).astype(jnp.float32)
        start_rows = jnp.clip(block_tags[:, 0] - 1, 0, tile_rows - 1)
        start_cols = jnp.clip(block_tags[:, 1] - 1, 0, tile_cols - 1)
        patches = jax.vmap(
            lambda row_start, col_start: lax.dynamic_slice(
                padded, (zero_index, row_start, col_start), (2, M, M)
            )
        )(start_rows, start_cols)
        spread, part_real, part_imag, part_weight = pattern_terms(
            probe_field, patches, block_rows, live_mask, cosine_table, sine_table
        )
        accumulated = add_patches(accumulated, spread, start_rows, start_cols)
        return (accumulated, grad_real + part_real, grad_imag + part_imag, weight + part_weight)

    start_state = (
        jnp.zeros((3, tile_rows + M, tile_cols + M), jnp.float32),
        jnp.zeros((M, M), jnp.float32),
        jnp.zeros((M, M), jnp.float32),
        jnp.zeros((M, M), jnp.float32),
    )
    accumulated, grad_real, grad_imag, weight = lax.fori_loop(
        0, block_turns, one_block, start_state
    )
    for direction in (1, -1):
        rim_strip = (
            accumulated[:, tile_rows + rim_width :, :]
            if direction == 1
            else accumulated[:, :rim_width, :]
        )
        arrived = from_behind(rim_strip, "ty", direction)
        if direction == 1:
            accumulated = accumulated.at[:, rim_width : 2 * rim_width, :].add(arrived)
        else:
            accumulated = accumulated.at[:, tile_rows : tile_rows + rim_width, :].add(arrived)
    for direction in (1, -1):
        rim_strip = (
            accumulated[:, :, tile_cols + rim_width :]
            if direction == 1
            else accumulated[:, :, :rim_width]
        )
        arrived = from_behind(rim_strip, "tx", direction)
        if direction == 1:
            accumulated = accumulated.at[:, :, rim_width : 2 * rim_width].add(arrived)
        else:
            accumulated = accumulated.at[:, :, tile_cols : tile_cols + rim_width].add(arrived)
    interior = accumulated[:, rim_width : rim_width + tile_rows, rim_width : rim_width + tile_cols]
    new_object = object_field - interior[:2] / (interior[2] + floor_level)
    summed = lax.psum((grad_real, grad_imag, weight), ("ty", "tx"))
    new_probe = probe_field - jnp.stack([summed[0], summed[1]]) / (summed[2] + tiny_level)
    return (new_object, new_probe)


def solution(mesh):
    placed = (
        P("ty", "tx", None, None, None),
        P("ty", "tx", None, None),
        P("ty", "tx", None),
        P("ty", "tx"),
        P(None, "ty", "tx"),
        P(),
    )
    return jax.shard_map(
        shards, mesh=mesh, in_specs=placed, out_specs=(P(None, "ty", "tx"), P()), check_vma=False
    )
```

profile of v0, /device:TPU:1, one launch (start us, length us, event | category | flops | bytes accessed | tf_op | source)
XLA Modules:
  0.0 1039.0 jit_solution(12287225430988321243)
XLA Ops:
  24.3 4.9 collective-permute-start.3
  69.9 4.3 collective-permute-start.10
  74.2 5.3 collective-permute-start.26
  79.6 5.7 collective-permute-start.19
  105.3 4.3 collective-permute-start.11
  117.8 4.2 collective-permute-start.25
  131.0 7.0 collective-permute-start.22
  155.1 5.0 collective-permute-done.15
  163.8 4.6 copy.126
  170.9 400.0 %while.52 = (s32[]{:T(128)}, f32[3,640,640]{2,1,0:T(8,128)}, f32[128,128]{1,0:T(8,128)S(1)}, f32[128,128]{1,0:T(8,128)S(1)}, f32[128,128]{1,0:T(8,128)S(1)}, /*i...) while((s32[]{:T(128)}, f32[3,640,640]{2,1,0:T(8,128)}, ...), condition=%wide.region_16.20_spmd.clone.clone, body=%wide.region_10.19_spmd.clone.clone.sunk | while | flops 3232875776 | bytes 34477920 | solution.py:184
  175.1 24.4 %while.53 = (s32[]{:T(128)}, f32[2,640,640]{2,1,0:T(8,128)}, s32[8,3]{1,0:T(8,128)S(1)}, f32[8,2,128,128]{3,2,0,1:T(8,128)S(1)}, s32[]{:T(128)}) while((s32[]{:T(128)}, f32[2,640,640]{2,1,0:T(8,128)}, s32[8,3]{1,0:T(8,128)S(1)}, f32[8,2,128,128]{3,2,0,1:T(8,128)S(1)}, s32[]{:T(128)}) %tuple.186), condition=%wide.while_cond.4, body=%wide.while_body.4.sunk | while | flops 2 | bytes 262269 | solution.py:168
  218.6 85.7 %while.54 = (s32[]{:T(128)}, f32[3,640,640]{2,1,0:T(8,128)}, s32[8]{0:T(128)S(1)}, s32[8]{0:T(128)S(1)}, f32[8,3,128,128]{3,2,0,1:T(8,128)S(1)}, /*index=5*/s32[]{:T(128)}, s32[]{:T(128)}, s32[]{:T(128)}) while((s32[]{:T(128)}, f32[3,640,640]{2,1,0:T(8,128)}, s32[8]{0:T(128)S(1)}, s32[8]{0:T(128)S(1)}, f32[8,3,128,128]{3,2,0,1:T(8,128)S(1)}, ...), condition=%wide.region_12.15_spmd, body=%wide.region_11.14_spmd.sunk | while | flops 49160 | bytes 983241 | solution.py:98
  257.4 4.1 dynamic_update_slice.8
  289.5 4.1 dynamic_update_slice.8
  308.6 24.4 %while.53 = (s32[]{:T(128)}, f32[2,640,640]{2,1,0:T(8,128)}, s32[8,3]{1,0:T(8,128)S(1)}, f32[8,2,128,128]{3,2,0,1:T(8,128)S(1)}, s32[]{:T(128)}) while((s32[]{:T(128)}, f32[2,640,640]{2,1,0:T(8,128)}, s32[8,3]{1,0:T(8,128)S(1)}, f32[8,2,128,128]{3,2,0,1:T(8,128)S(1)}, s32[]{:T(128)}) %tuple.186), condition=%wide.while_cond.4, body=%wide.while_body.4.sunk | while | flops 2 | bytes 262269 | solution.py:168
  352.1 85.7 %while.54 = (s32[]{:T(128)}, f32[3,640,640]{2,1,0:T(8,128)}, s32[8]{0:T(128)S(1)}, s32[8]{0:T(128)S(1)}, f32[8,3,128,128]{3,2,0,1:T(8,128)S(1)}, /*index=5*/s32[]{:T(128)}, s32[]{:T(128)}, s32[]{:T(128)}) while((s32[]{:T(128)}, f32[3,640,640]{2,1,0:T(8,128)}, s32[8]{0:T(128)S(1)}, s32[8]{0:T(128)S(1)}, f32[8,3,128,128]{3,2,0,1:T(8,128)S(1)}, ...), condition=%wide.region_12.15_spmd, body=%wide.region_11.14_spmd.sunk | while | flops 49160 | bytes 983241 | solution.py:98
  369.4 4.1 dynamic_update_slice.8
  390.9 4.1 dynamic_update_slice.8
  401.6 4.1 dynamic_update_slice.8
  442.0 24.4 %while.53 = (s32[]{:T(128)}, f32[2,640,640]{2,1,0:T(8,128)}, s32[8,3]{1,0:T(8,128)S(1)}, f32[8,2,128,128]{3,2,0,1:T(8,128)S(1)}, s32[]{:T(128)}) while((s32[]{:T(128)}, f32[2,640,640]{2,1,0:T(8,128)}, s32[8,3]{1,0:T(8,128)S(1)}, f32[8,2,128,128]{3,2,0,1:T(8,128)S(1)}, s32[]{:T(128)}) %tuple.186), condition=%wide.while_cond.4, body=%wide.while_body.4.sunk | while | flops 2 | bytes 262269 | solution.py:168
  485.5 85.3 %while.54 = (s32[]{:T(128)}, f32[3,640,640]{2,1,0:T(8,128)}, s32[8]{0:T(128)S(1)}, s32[8]{0:T(128)S(1)}, f32[8,3,128,128]{3,2,0,1:T(8,128)S(1)}, /*index=5*/s32[]{:T(128)}, s32[]{:T(128)}, s32[]{:T(128)}) while((s32[]{:T(128)}, f32[3,640,640]{2,1,0:T(8,128)}, s32[8]{0:T(128)S(1)}, s32[8]{0:T(128)S(1)}, f32[8,3,128,128]{3,2,0,1:T(8,128)S(1)}, ...), condition=%wide.region_12.15_spmd, body=%wide.region_11.14_spmd.sunk | while | flops 49160 | bytes 983241 | solution.py:98
  534.5 4.1 dynamic_update_slice.8
  545.2 4.1 dynamic_update_slice.8
  556.0 4.1 dynamic_update_slice.8
  566.7 4.1 dynamic_update_slice.8
  573.9 134.2 %collective-permute-done.28 = f32[3,64,640]{2,1,0:T(8,128)S(1)} collective-permute-done((f32[3,64,640]{2,1,0:T(8,128)S(1)}, f32[3,64,640]{2,1,0:T(8,128)S(1)}, u32[]{:S(2)}, u32[]{:S(2)}) %collective-permute-start.28) | collective-permute-done | bytes 491552 | tf_op jit(solution)/shard_map/ppermute | solution.py:34
  713.1 8.1 collective-permute-done.29
  725.0 13.6 %collective-permute-start.30 = (f32[3,640,64]{1,2,0:T(8,128)S(1)}, f32[3,640,64]{1,2,0:T(8,128)S(1)}, u32[]{:S(2)}, u32[]{:S(2)}) collective-permute-start(f32[3,640,64]{1,2,0:T(8,128)S(1)} %copy.127), channel_id=1, source_target_pairs={{0,1},{1,2},{2,3},{3,4},{4,5},{5,6},{6,7},{7,8},{8,9},{9,10},{10,1... | collective-permute-start | bytes 1474568 | tf_op jit(solution)/shard_map/ppermute | solution.py:34
  738.6 5.7 collective-permute-done.30
  746.2 9.2 scatter-add.16
  758.2 256.2 %all-reduce.3.cloned.1.call-done = (f32[1,128,128]{2,1,0:T(8,128)}, f32[1,128,128]{2,1,0:T(8,128)}, f32[128,128]{1,0:T(8,128)}) async-done(((f32[1,128,128]{2,1,0:T(8,128)}, f32[1,128,128]{2,1,0:T(8,128)}, f32[128,128]{1,0:T(8,128)}), (f32[1,128,128]{2,1,0:T(8,128)}, f32[1,128,128]{2,1,0:T(8,128)}, f32[128,128]{1,0:T(8,128)})) %all-reduce.3.cloned.1.call-update) | async-done | bytes 196624 | tf_op jit(solution)/shard_map/psum | solution.py:211
  1019.8 7.0 scatter-add.19
  (461 shorter events, 405.6 us)
Async XLA Ops:
  7.2 1007.2 %all-reduce.3.cloned.1.call-start = ((), (), s32[]{:S(2)}) async-start(), calls=%async_computation | async-start | bytes 393216 | tf_op jit(solution)/shard_map/psum | solution.py:211
  13.9 65.7 %collective-permute-start = (s32[2,3]{1,0:T(2,128)S(1)}, s32[2,3]{1,0:T(2,128)}, u32[]{:S(2)}, u32[]{:S(2)}) collective-permute-start(s32[2,3]{1,0:T(2,128)S(1)} %select_select_fusion.7), channel_id=1, source_target_pairs={{1,0},{2,1},{3,2},{4,3},{5,4},{6,5},{7,6},{8,7},{9,8},{10,9},{11,1... | collective-permute-start | bytes 80 | tf_op jit(solution)/shard_map/ppermute | solution.py:34
  16.5 48.0 %collective-permute-start.2 = (s32[2,3]{1,0:T(2,128)S(1)}, s32[2,3]{1,0:T(2,128)S(1)}, u32[]{:S(2)}, u32[]{:S(2)}) collective-permute-start(s32[2,3]{1,0:T(2,128)S(1)} %select_select_fusion.6), channel_id=1, source_target_pairs={{16,0},{32,16},{48,32},{64,48},{80,64},{96,80},{112,96},{17,1},{33... | collective-permute-start | bytes 80 | tf_op jit(solution)/shard_map/ppermute | solution.py:34
  24.3 61.1 %collective-permute-start.3 = (s32[2,3]{1,0:T(2,128)S(1)}, s32[2,3]{1,0:T(2,128)}, u32[]{:S(2)}, u32[]{:S(2)}) collective-permute-start(s32[2,3]{1,0:T(2,128)S(1)} %select_select_fusion.5), channel_id=1, source_target_pairs={{0,1},{1,2},{2,3},{3,4},{4,5},{5,6},{6,7},{7,8},{8,9},{9,10},{10,1... | collective-permute-start | bytes 80 | tf_op jit(solution)/shard_map/ppermute | solution.py:34
  30.4 35.4 %collective-permute-start.5 = (s32[2,3]{1,0:T(2,128)S(1)}, s32[2,3]{1,0:T(2,128)S(1)}, u32[]{:S(2)}, u32[]{:S(2)}) collective-permute-start(s32[2,3]{1,0:T(2,128)S(1)} %select_select_fusion.4), channel_id=1, source_target_pairs={{1,0},{2,1},{3,2},{4,3},{5,4},{6,5},{7,6},{8,7},{9,8},{10,9},{11,1... | collective-permute-start | bytes 80 | tf_op jit(solution)/shard_map/ppermute | solution.py:34
  36.8 33.0 %collective-permute-start.6 = (s32[2,3]{1,0:T(2,128)}, s32[2,3]{1,0:T(2,128)S(1)}, u32[]{:S(2)}, u32[]{:S(2)}) collective-permute-start(s32[2,3]{1,0:T(2,128)} %select_select_fusion.3), channel_id=1, source_target_pairs={{0,1},{1,2},{2,3},{3,4},{4,5},{5,6},{6,7},{7,8},{8,9},{9,10},{10,1... | collective-permute-start | bytes 80 | tf_op jit(solution)/shard_map/ppermute | solution.py:34
  64.4 32.5 %collective-permute-start.7 = (s32[2,3]{1,0:T(2,128)S(1)}, s32[2,3]{1,0:T(2,128)S(1)}, u32[]{:S(2)}, u32[]{:S(2)}) collective-permute-start(s32[2,3]{1,0:T(2,128)S(1)} %select_select_fusion.2), channel_id=1, source_target_pairs={{1,0},{2,1},{3,2},{4,3},{5,4},{6,5},{7,6},{8,7},{9,8},{10,9},{11,1... | collective-permute-start | bytes 80 | tf_op jit(solution)/shard_map/ppermute | solution.py:34
  65.8 8.4 collective-permute-start.9
  69.9 29.0 %collective-permute-start.10 = (s32[2,3]{1,0:T(2,128)S(1)}, s32[2,3]{1,0:T(2,128)S(1)}, u32[]{:S(2)}, u32[]{:S(2)}) collective-permute-start(s32[2,3]{1,0:T(2,128)S(1)} %select_select_fusion), channel_id=1, source_target_pairs={{0,1},{1,2},{2,3},{3,4},{4,5},{5,6},{6,7},{7,8},{8,9},{9,10},{10,1... | collective-permute-start | bytes 80 | tf_op jit(solution)/shard_map/ppermute | solution.py:34
  74.2 56.7 %collective-permute-start.26 = (f32[2,128,128]{2,1,0:T(8,128)}, f32[2,128,128]{2,1,0:T(8,128)}, u32[]{:S(2)}, u32[]{:S(2)}) collective-permute-start(f32[2,128,128]{2,1,0:T(8,128)} %broadcast_select_fusion.1), channel_id=1, source_target_pairs={{0,1},{1,2},{2,3},{3,4},{4,5},{5,6},{6,7},{7,8},{8,9},{9,10},{10,1... | collective-permute-start | bytes 393224 | tf_op jit(solution)/shard_map/ppermute | solution.py:34
  79.6 45.5 %collective-permute-start.19 = (f32[2,128,128]{2,1,0:T(8,128)}, f32[2,128,128]{2,1,0:T(8,128)}, u32[]{:S(2)}, u32[]{:S(2)}) collective-permute-start(f32[2,128,128]{2,1,0:T(8,128)} %broadcast_select_fusion.6), channel_id=1, source_target_pairs={{0,1},{1,2},{2,3},{3,4},{4,5},{5,6},{6,7},{7,8},{8,9},{9,10},{10,1... | collective-permute-start | bytes 393224 | tf_op jit(solution)/shard_map/ppermute | solution.py:34
  85.3 5.1 collective-permute-start.1
  90.4 5.1 collective-permute-start.4
  95.5 16.9 %collective-permute-start.16 = (f32[2,128,128]{2,1,0:T(8,128)}, f32[2,128,128]{2,1,0:T(8,128)}, u32[]{:S(2)}, u32[]{:S(2)}) collective-permute-start(f32[2,128,128]{2,1,0:T(8,128)} %broadcast_select_fusion.8), channel_id=1, source_target_pairs={{1,0},{2,1},{3,2},{4,3},{5,4},{6,5},{7,6},{8,7},{9,8},{10,9},{11,1... | collective-permute-start | bytes 393224 | tf_op jit(solution)/shard_map/ppermute | solution.py:34
  96.9 20.9 %collective-permute-start.12 = (f32[2,64,512]{1,2,0:T(8,128)}, f32[2,64,512]{1,2,0:T(8,128)S(1)}, u32[]{:S(2)}, u32[]{:S(2)}) collective-permute-start(f32[2,64,512]{1,2,0:T(8,128)} %get-tuple-element.723), channel_id=1, source_target_pairs={{0,16},{16,32},{32,48},{48,64},{64,80},{80,96},{96,112},{1,17},{17... | collective-permute-start | bytes 786440 | tf_op jit(solution)/shard_map/ppermute | solution.py:25
  98.9 6.4 collective-permute-start.8
  110.3 11.7 %collective-permute-start.13 = (f32[2,64,512]{1,2,0:T(8,128)}, f32[2,64,512]{1,2,0:T(8,128)}, u32[]{:S(2)}, u32[]{:S(2)}) collective-permute-start(f32[2,64,512]{1,2,0:T(8,128)} %get-tuple-element.724), channel_id=1, source_target_pairs={{16,0},{32,16},{48,32},{64,48},{80,64},{96,80},{112,96},{17,1},{33... | collective-permute-start | bytes 786440 | tf_op jit(solution)/shard_map/ppermute | solution.py:26
  112.4 14.0 %collective-permute-start.17 = (f32[2,128,128]{2,1,0:T(8,128)}, f32[2,128,128]{2,1,0:T(8,128)S(1)}, u32[]{:S(2)}, u32[]{:S(2)}) collective-permute-start(f32[2,128,128]{2,1,0:T(8,128)} %collective-permute-done.16), channel_id=1, source_target_pairs={{16,0},{32,16},{48,32},{64,48},{80,64},{96,80},{112,96},{17,1},{33... | collective-permute-start | bytes 393224 | tf_op jit(solution)/shard_map/ppermute | solution.py:34
  117.8 33.8 %collective-permute-start.25 = (f32[2,128,128]{2,1,0:T(8,128)S(1)}, f32[2,128,128]{2,1,0:T(8,128)S(1)}, u32[]{:S(2)}, u32[]{:S(2)}) collective-permute-start(f32[2,128,128]{2,1,0:T(8,128)S(1)} %broadcast_select_fusion.2), channel_id=1, source_target_pairs={{0,16},{16,32},{32,48},{48,64},{64,80},{80,96},{96,112},{1,17},{17... | collective-permute-start | bytes 393224 | tf_op jit(solution)/shard_map/ppermute | solution.py:34
  122.0 7.0 collective-permute-start.18
  125.1 12.9 %collective-permute-start.23 = (f32[2,128,128]{2,1,0:T(8,128)S(1)}, f32[2,128,128]{2,1,0:T(8,128)S(1)}, u32[]{:S(2)}, u32[]{:S(2)}) collective-permute-start(f32[2,128,128]{2,1,0:T(8,128)S(1)} %broadcast_select_fusion.3), channel_id=1, source_target_pairs={{1,0},{2,1},{3,2},{4,3},{5,4},{6,5},{7,6},{8,7},{9,8},{10,9},{11,1... | collective-permute-start | bytes 393224 | tf_op jit(solution)/shard_map/ppermute | solution.py:34
  126.4 15.5 %collective-permute-start.20 = (f32[2,128,128]{2,1,0:T(8,128)}, f32[2,128,128]{2,1,0:T(8,128)S(1)}, u32[]{:S(2)}, u32[]{:S(2)}) collective-permute-start(f32[2,128,128]{2,1,0:T(8,128)} %collective-permute-done.19), channel_id=1, source_target_pairs={{16,0},{32,16},{48,32},{64,48},{80,64},{96,80},{112,96},{17,1},{33... | collective-permute-start | bytes 393224 | tf_op jit(solution)/shard_map/ppermute | solution.py:34
  129.0 15.7 %collective-permute-start.21 = (f32[2,128,128]{2,1,0:T(8,128)}, f32[2,128,128]{2,1,0:T(8,128)S(1)}, u32[]{:S(2)}, u32[]{:S(2)}) collective-permute-start(f32[2,128,128]{2,1,0:T(8,128)} %broadcast_select_fusion.5), channel_id=1, source_target_pairs={{1,0},{2,1},{3,2},{4,3},{5,4},{6,5},{7,6},{8,7},{9,8},{10,9},{11,1... | collective-permute-start | bytes 393224 | tf_op jit(solution)/shard_map/ppermute | solution.py:34
  131.0 18.1 %collective-permute-start.22 = (f32[2,128,128]{2,1,0:T(8,128)}, f32[2,128,128]{2,1,0:T(8,128)S(1)}, u32[]{:S(2)}, u32[]{:S(2)}) collective-permute-start(f32[2,128,128]{2,1,0:T(8,128)} %broadcast_select_fusion.4), channel_id=1, source_target_pairs={{0,1},{1,2},{2,3},{3,4},{4,5},{5,6},{6,7},{7,8},{8,9},{9,10},{10,1... | collective-permute-start | bytes 393224 | tf_op jit(solution)/shard_map/ppermute | solution.py:34
  138.0 14.3 %collective-permute-start.27 = (f32[2,128,128]{2,1,0:T(8,128)}, f32[2,128,128]{2,1,0:T(8,128)S(1)}, u32[]{:S(2)}, u32[]{:S(2)}) collective-permute-start(f32[2,128,128]{2,1,0:T(8,128)} %collective-permute-done.26), channel_id=1, source_target_pairs={{0,16},{16,32},{32,48},{48,64},{64,80},{80,96},{96,112},{1,17},{17... | collective-permute-start | bytes 393224 | tf_op jit(solution)/shard_map/ppermute | solution.py:34
  141.9 9.1 collective-permute-start.24
  144.7 10.4 collective-permute-start.14
  149.0 11.1 %collective-permute-start.15 = (f32[2,640,64]{1,2,0:T(8,128)S(1)}, f32[2,640,64]{1,2,0:T(8,128)S(1)}, u32[]{:S(2)}, u32[]{:S(2)}) collective-permute-start(f32[2,640,64]{1,2,0:T(8,128)S(1)} %get-tuple-element.722), channel_id=1, source_target_pairs={{1,0},{2,1},{3,2},{4,3},{5,4},{6,5},{7,6},{8,7},{9,8},{10,9},{11,1... | collective-permute-start | bytes 983048 | tf_op jit(solution)/shard_map/ppermute | solution.py:26
  572.0 136.1 %collective-permute-start.28 = (f32[3,64,640]{2,1,0:T(8,128)S(1)}, f32[3,64,640]{2,1,0:T(8,128)S(1)}, u32[]{:S(2)}, u32[]{:S(2)}) collective-permute-start(f32[3,64,640]{2,1,0:T(8,128)S(1)} %slice.224), channel_id=1, source_target_pairs={{0,16},{16,32},{32,48},{48,64},{64,80},{80,96},{96,112},{1,17},{17... | collective-permute-start | bytes 1474568 | tf_op jit(solution)/shard_map/ppermute | solution.py:34
  711.1 10.1 collective-permute-start.29
  725.0 19.3 %collective-permute-start.30 = (f32[3,640,64]{1,2,0:T(8,128)S(1)}, f32[3,640,64]{1,2,0:T(8,128)S(1)}, u32[]{:S(2)}, u32[]{:S(2)}) collective-permute-start(f32[3,640,64]{1,2,0:T(8,128)S(1)} %copy.127), channel_id=1, source_target_pairs={{0,1},{1,2},{2,3},{3,4},{4,5},{5,6},{6,7},{7,8},{8,9},{9,10},{10,1... | collective-permute-start | bytes 1474568 | tf_op jit(solution)/shard_map/ppermute | solution.py:34
  756.9 259.9 %collective-permute-start.31 = (f32[3,640,64]{1,2,0:T(8,128)S(1)}, f32[3,640,64]{1,2,0:T(8,128)S(1)}, u32[]{:S(2)}, u32[]{:S(2)}) collective-permute-start(f32[3,640,64]{1,2,0:T(8,128)S(1)} %copy.129), channel_id=1, source_target_pairs={{1,0},{2,1},{3,2},{4,3},{5,4},{6,5},{7,6},{8,7},{9,8},{10,9},{11,1... | collective-permute-start | bytes 1474568 | tf_op jit(solution)/shard_map/ppermute | solution.py:34
  (9 other events, 527.1 us)
Sparse Core Ops, SparseCore 0:
  738.7 275.6 all-reduce.2
where the time goes:
time: 1050 us; the launch traced here: 1040 us
  waiting for transfers between devices  421 us (40%)
  local copies, waits for them, and re-layouts  270 us (26%)
  starting transfers between devices  101 us (10%)
  loops' own time  101 us (10%)
  other arithmetic  73.1 us (7%)
  matrix products  56.2 us (5%)
  between operations  16.2 us (2%)
    psum x1, waiting for transfers between devices, shards(): summed = lax.psum((grad_real, grad_imag, weight), ('ty', 'tx'))  256 us
    ppermute x28, waiting for transfers between devices, from_behind(): return lax.ppermute(block, axis, route)  158 us
    another operation x3, loops' own time, add_patches(): return lax.fori_loop(0, spread.shape[0], add_one, accumulated)  100 us
    dynamic_update_slice x24, local copies, waits for them, and re-layouts, add_one(): lax.dynamic_update_slice(current, window + spread[patch_id], (zero_index,...  96.8 us
    ppermute x28, starting transfers between devices, from_behind(): return lax.ppermute(block, axis, route)  92.5 us
    gather x72, local copies, waits for them, and re-layouts  72.6 us
    add x24, other arithmetic, add_one(): window + spread[patch_id]  27.6 us
  transfers between devices with their start and end apart: 33, of which 10 were waited for; matrix products, arithmetic and copies ran while one was open for 6% of the time, Pallas kernels for 0%

commit v1 on v0

v1 whole, which is shorter than its diff:
```python
import functools

import jax
import jax.numpy as jnp
import numpy as np
from jax import lax
from jax.experimental import pallas as pl
from jax.experimental.pallas import tpu as pltpu
from jax.sharding import PartitionSpec as P

M = 128
MOVE = 2
RIM = M // 2
LANES = 128
BATCH = 4

offset_level = 1.0
floor_level = 1.0
tiny_level = 1e-06

MESH_ID = pl.DeviceIdType.MESH
DIRECTIONS = [(-1, -1), (-1, 0), (-1, 1), (0, -1), (0, 1), (1, -1), (1, 0), (1, 1)]
CORNERS = [(-1, -1), (-1, 1), (1, -1), (1, 1)]

F32 = jnp.float32
BF16 = jnp.bfloat16
I32 = jnp.int32


def in_vmem():
    return pl.BlockSpec(memory_space=pltpu.VMEM)


def in_smem():
    return pl.BlockSpec(memory_space=pltpu.SMEM)


def anywhere():
    return pl.BlockSpec(memory_space=pl.ANY)


def dft_tables():
    phase = (np.outer(np.arange(M), np.arange(M)) % M) * (2.0 * np.pi / M)
    c, s = np.cos(phase) / np.sqrt(M), -np.sin(phase) / np.sqrt(M)
    forward = np.block([[c, s], [-s, c]])
    tables = []
    for table in (forward, forward.T):
        high = table.astype(BF16)
        tables += [high, (table - high.astype(np.float64)).astype(BF16)]
    return tables


def lane_ids(rows):
    return lax.broadcasted_iota(I32, (rows, LANES), 1)


def neighbour(down, right):
    ty, tx = lax.axis_index("ty"), lax.axis_index("tx")
    n_ty, n_tx = lax.axis_size("ty"), lax.axis_size("tx")
    return lax.rem(ty + (down + n_ty), n_ty), lax.rem(tx + (right + n_tx), n_tx)


def is_inside(down, right):
    ty, tx = lax.axis_index("ty"), lax.axis_index("tx")
    row, col = ty + down, tx + right
    return (row >= 0) & (row < lax.axis_size("ty")) & (col >= 0) & (col < lax.axis_size("tx"))


def pack_left(first, second, rows):
    return jnp.where(lane_ids(rows) >= RIM, first, pltpu.roll(second, RIM, 1))


def pack_right(first, second, rows):
    return jnp.where(lane_ids(rows) < RIM, first, pltpu.roll(second, RIM, 1))


def spread_kernel(
    owners_ref,
    positions_ref,
    counts_ref,
    measured_ref,
    object_ref,
    pattern_out,
    tag_out,
    side_out,
    row_out,
    corner_out,
    pattern_pack,
    tag_pack,
    side_pack,
    send_sem,
    recv_sem,
):
    slots = measured_ref.shape[0]
    rows, cols = object_ref.shape[1:]
    n_tx = lax.axis_size("tx")
    ty, tx = lax.axis_index("ty"), lax.axis_index("tx")

    barrier = pltpu.get_barrier_semaphore()
    for down, right in DIRECTIONS:
        pl.semaphore_signal(barrier, inc=1, device_id=neighbour(down, right), device_id_type=MESH_ID)
    edge = pl.ds(cols - LANES, LANES)
    side_pack[0] = pack_left(object_ref[0, :, edge], object_ref[1, :, edge], rows)
    side_pack[1] = pack_right(object_ref[0, :, :LANES], object_ref[1, :, :LANES], rows)
    pl.semaphore_wait(barrier, len(DIRECTIONS))

    copies = []

    def send(source, target, down, right):
        slot = len(copies)
        copy = pltpu.make_async_remote_copy(
            src_ref=source,
            dst_ref=target,
            send_sem=send_sem.at[slot],
            recv_sem=recv_sem.at[slot],
            device_id=neighbour(down, right),
            device_id_type=MESH_ID,
        )
        copy.start()
        copies.append(copy)

    send(side_pack.at[0], side_out.at[0], 0, 1)
    send(side_pack.at[1], side_out.at[1], 0, -1)
    send(object_ref.at[:, pl.ds(rows - RIM, RIM), :], row_out.at[0], 1, 0)
    send(object_ref.at[:, pl.ds(0, RIM), :], row_out.at[1], -1, 0)
    for corner, (down, right) in enumerate(CORNERS):
        source = side_pack.at[0 if right == 1 else 1, pl.ds(0 if down == -1 else rows - RIM, RIM), :]
        send(source, corner_out.at[corner], down, right)

    count = counts_ref[0, 0]
    lane = lane_ids(1)
    for way, (down, right) in enumerate(DIRECTIONS):
        target = jnp.where(is_inside(down, right), (ty + down) * n_tx + (tx + right), -1)
        found, first, second = jnp.int32(0), jnp.int32(0), jnp.int32(0)
        for slot in range(slots):
            hit = (owners_ref[0, 0, slot] == target) & (slot < count)
            first = jnp.where(hit & (found == 0), slot, first)
            second = jnp.where(hit & (found == 1), slot, second)
            found = found + hit.astype(I32)
        tag = jnp.zeros((1, LANES), I32)
        for index, chosen in enumerate((first, second)):
            pattern_pack[way, index] = measured_ref[chosen]
            valid = (found > index).astype(I32)
            tag = jnp.where(lane == 3 * index, valid, tag)
            tag = jnp.where(lane == 3 * index + 1, positions_ref[0, 0, chosen, 0], tag)
            tag = jnp.where(lane == 3 * index + 2, positions_ref[0, 0, chosen, 1], tag)
        tag_pack[way] = tag
    for way, (down, right) in enumerate(DIRECTIONS):
        send(tag_pack.at[way], tag_out.at[way], down, right)
        send(pattern_pack.at[way], pattern_out.at[way], down, right)
    for copy in copies:
        copy.wait()


def spread(owners, positions, counts, measured, object_field):
    rows, cols = object_field.shape[1:]
    ways = len(DIRECTIONS)
    copies = 4 + len(CORNERS) + 2 * ways
    return pl.pallas_call(
        spread_kernel,
        out_shape=(
            jax.ShapeDtypeStruct((ways, MOVE, M, M), F32),
            jax.ShapeDtypeStruct((ways, 1, LANES), I32),
            jax.ShapeDtypeStruct((2, rows, LANES), F32),
            jax.ShapeDtypeStruct((2, 2, RIM, cols), F32),
            jax.ShapeDtypeStruct((len(CORNERS), RIM, LANES), F32),
        ),
        in_specs=[in_smem(), in_smem(), in_smem(), in_vmem(), in_vmem()],
        out_specs=(anywhere(),) * 5,
        scratch_shapes=[
            pltpu.VMEM((ways, MOVE, M, M), F32),
            pltpu.VMEM((ways, 1, LANES), I32),
            pltpu.VMEM((2, rows, LANES), F32),
            pltpu.SemaphoreType.DMA((copies,)),
            pltpu.SemaphoreType.DMA((copies,)),
        ],
        compiler_params=pltpu.CompilerParams(
            collective_id=0, has_side_effects=True, vmem_limit_bytes=16 << 20
        ),
        name="spread",
    )(owners, positions, counts, measured, object_field)


PADDED_BLOCKS = 2


def split(value):
    high = value.astype(BF16)
    return high, (value - high.astype(F32)).astype(BF16)


def dot(a, b):
    return jnp.dot(a, b, preferred_element_type=F32)


def patterns_kernel(
    owners_ref,
    positions_ref,
    counts_ref,
    tag_ref,
    measured_ref,
    arrived_ref,
    object_ref,
    side_ref,
    row_ref,
    corner_ref,
    probe_ref,
    uh_ref,
    ul_ref,
    vh_ref,
    vl_ref,
    sums_ref,
    left_ref,
    right_ref,
    probe_sums_ref,
    field,
    shifted,
    turned_sums,
    data,
    window,
    framed,
    xh,
    xl,
    yh,
    yl,
    row_list,
    col_list,
    data_list,
    copy_sem,
):
    slots = owners_ref.shape[2]
    rows, cols = object_ref.shape[1:]
    blocks = cols // LANES
    n_tx = lax.axis_size("tx")
    ty, tx = lax.axis_index("ty"), lax.axis_index("tx")
    self_index = ty * n_tx + tx
    moved = 2 * len(DIRECTIONS)

    own_copy = pltpu.make_async_copy(measured_ref, data.at[pl.ds(0, slots)], copy_sem.at[0])
    own_copy.start()
    moved_copy = pltpu.make_async_copy(arrived_ref, data.at[pl.ds(slots, moved)], copy_sem.at[1])
    moved_copy.start()

    for part in range(2):
        for block in range(blocks):
            field[part, 1 + block, RIM : RIM + rows, :] = object_ref[part, :, block * LANES : (block + 1) * LANES]
            field[part, 1 + block, :RIM, :] = jnp.where(
                is_inside(-1, 0), row_ref[0, part, :, block * LANES : (block + 1) * LANES], 0.0
            )
            field[part, 1 + block, RIM + rows :, :] = jnp.where(
                is_inside(1, 0), row_ref[1, part, :, block * LANES : (block + 1) * LANES], 0.0
            )

    def unpacked(part, value):
        return value if part == 0 else pltpu.roll(value, RIM, 1)

    for part in range(2):
        field[part, 0, RIM : RIM + rows, :] = jnp.where(is_inside(0, -1), unpacked(part, side_ref[0]), 0.0)
        field[part, 1 + blocks, RIM : RIM + rows, :] = jnp.where(is_inside(0, 1), unpacked(part, side_ref[1]), 0.0)
        for corner, (down, right) in enumerate(CORNERS):
            here = pl.ds(0, RIM) if down == 1 else pl.ds(RIM + rows, RIM)
            field[part, 0 if right == 1 else 1 + blocks, here, :] = jnp.where(
                is_inside(-down, -right), unpacked(part, corner_ref[corner]), 0.0
            )

    for turn in range(8):
        for part in range(2):
            value = probe_ref[part]
            shifted[turn, part] = pltpu.roll(value, turn, 0) if turn else value
    sums_ref[...] = jnp.zeros(sums_ref.shape, F32)
    turned_sums[...] = jnp.zeros(turned_sums.shape, F32)

    count = counts_ref[0, 0]

    def own(slot, total):
        row_list[total] = positions_ref[0, 0, slot, 0]
        col_list[total] = positions_ref[0, 0, slot, 1]
        data_list[total] = slot
        return total + ((owners_ref[0, 0, slot] == self_index) & (slot < count)).astype(I32)

    total = lax.fori_loop(0, slots, own, jnp.int32(0))
    for way in range(len(DIRECTIONS)):
        for index in range(MOVE):
            row_list[total] = tag_ref[way, 0, 3 * index + 1]
            col_list[total] = tag_ref[way, 0, 3 * index + 2]
            data_list[total] = slots + way * MOVE + index
            total = total + tag_ref[way, 0, 3 * index]
    for index in range(BATCH):
        row_list[total + index] = 0
        col_list[total + index] = 0
        data_list[total + index] = 0

    own_copy.wait()
    moved_copy.wait()
    lane_of_frame = lane_ids(M)
    lane_of_window = lane_ids(M + 8)
    row_of_tile = lax.broadcasted_iota(I32, (8, LANES), 0)

    def place(step, index):
        number = step * BATCH + index
        row, col = row_list[number], col_list[number] + RIM
        turn, lane = row & 7, col & (LANES - 1)
        return number, pl.multiple_of(row - turn, 8), lax.shift_right_logical(col, 7), turn, lane

    def one_batch(step, _):
        for index in range(BATCH):
            _, row, block, turn, lane = place(step, index)
            later = lane_of_window >= lane
            kept = row_of_tile >= turn
            parts = []
            for part in range(2):
                here = field[part, block, pl.ds(row, M + 8), :]
                beside = field[part, block + 1, pl.ds(row, M + 8), :]
                value = jnp.where(later, here, beside)
                value = jnp.concatenate([jnp.where(kept, value[:8], value[M:]), value[8:M]], axis=0)
                window[index, part] = value
                parts.append(value)
            wr, wi = parts
            pr = pltpu.roll(shifted[turn, 0], lane, 1)
            pi = pltpu.roll(shifted[turn, 1], lane, 1)
            framed[index, 0] = pr
            framed[index, 1] = pi
            at = pl.ds(index * M, M)
            for part, value in enumerate((pr * wr - pi * wi, pr * wi + pi * wr)):
                xh[at, part * M : (part + 1) * M], xl[at, part * M : (part + 1) * M] = split(value)

        def right_product(high, low):
            a = xh[...]
            return dot(a, high[...]) + dot(xl[...], high[...]) + dot(a, low[...])

        def to_pairs(value):
            for index in range(BATCH):
                for part in range(2):
                    piece = value[index * M : (index + 1) * M, part * M : (part + 1) * M]
                    to = (index // 2, pl.ds(part * M, M), pl.ds((index % 2) * M, M))
                    yh[to], yl[to] = split(piece)

        def left_product(pair, high, low):
            return dot(high[...], yh[pair]) + dot(high[...], yl[pair]) + dot(low[...], yh[pair])

        to_pairs(right_product(uh_ref, ul_ref))
        for pair in range(BATCH // 2):
            far = left_product(pair, vh_ref, vl_ref)
            for half in range(2):
                index = 2 * pair + half
                fr = far[:M, half * M : (half + 1) * M]
                fi = far[M:, half * M : (half + 1) * M]
                number = step * BATCH + index
                ratio = 1.0 - data[data_list[number]] / (fr * fr + fi * fi + offset_level)
                at = pl.ds(index * M, M)
                for part, value in enumerate((fr * ratio, fi * ratio)):
                    xh[at, part * M : (part + 1) * M], xl[at, part * M : (part + 1) * M] = split(value)
        to_pairs(right_product(vh_ref, vl_ref))
        for pair in range(BATCH // 2):
            back = left_product(pair, uh_ref, ul_ref)
            for half in range(2):
                index = 2 * pair + half
                number, row, block, turn, lane = place(step, index)
                live = (number < total).astype(F32)
                cr = back[:M, half * M : (half + 1) * M] * live
                ci = back[M:, half * M : (half + 1) * M] * live
                wr, wi = window[index, 0], window[index, 1]
                pr, pi = framed[index, 0], framed[index, 1]
                back_lanes = (LANES - lane) & (LANES - 1)
                terms = (wr * cr + wi * ci, wr * ci - wi * cr, (wr * wr + wi * wi) * live)
                for kind, term in enumerate(terms):
                    turned_sums[turn, kind] += pltpu.roll(term, back_lanes, 1)
                later = lane_of_frame >= lane
                kept = row_of_tile >= turn
                terms = (pr * cr + pi * ci, pr * ci - pi * cr, (pr * pr + pi * pi) * live)
                for kind, term in enumerate(terms):
                    for beside in range(2):
                        piece = jnp.where(later, 0.0, term) if beside else jnp.where(later, term, 0.0)
                        top = piece[:8]
                        sums_ref[kind, block + beside, pl.ds(row + 8, M - 8), :] += piece[8:]
                        sums_ref[kind, block + beside, pl.ds(row, 8), :] += jnp.where(kept, top, 0.0)
                        sums_ref[kind, block + beside, pl.ds(row + M, 8), :] += jnp.where(kept, 0.0, top)
        return _

    lax.fori_loop(0, lax.div(total + (BATCH - 1), BATCH), one_batch, 0)

    for kind in range(3):
        total_of_kind = turned_sums[0, kind]
        for turn in range(1, 8):
            total_of_kind = total_of_kind + pltpu.roll(turned_sums[turn, kind], M - turn, 0)
        probe_sums_ref[kind] = total_of_kind

    half = rows // 2
    for pack, out, block in ((pack_left, left_ref, 0), (pack_right, right_ref, 1 + blocks)):
        def rim(kind, start, length):
            return sums_ref[kind, block, start : start + length, :]

        out[:rows, :] = pack(rim(0, RIM, rows), rim(1, RIM, rows), rows)
        out[rows : rows + half, :] = pack(rim(2, RIM, half), rim(2, RIM + half, half), half)
        at = rows + half
        for start in (0, RIM + rows):
            out[at : at + RIM, :] = pack(rim(0, start, RIM), rim(1, start, RIM), RIM)
            out[at + RIM : at + RIM + RIM // 2, :] = pack(
                rim(2, start, RIM // 2), rim(2, start + RIM // 2, RIM // 2), RIM // 2
            )
            at += RIM + RIM // 2


def patterns(owners, positions, counts, tags, measured, arrived, object_field, sides, edges, corners, probe):
    slots = measured.shape[0]
    rows, cols = object_field.shape[1:]
    blocks = cols // LANES + PADDED_BLOCKS
    moved = 2 * len(DIRECTIONS)
    packed = rows + rows // 2 + 3 * RIM
    entries = slots + moved + BATCH
    return pl.pallas_call(
        patterns_kernel,
        out_shape=(
            jax.ShapeDtypeStruct((3, blocks, rows + 2 * RIM, LANES), F32),
            jax.ShapeDtypeStruct((packed, LANES), F32),
            jax.ShapeDtypeStruct((packed, LANES), F32),
            jax.ShapeDtypeStruct((3, M, M), F32),
        ),
        in_specs=[in_smem()] * 4 + [anywhere()] * 2 + [in_vmem()] * 9,
        out_specs=(in_vmem(),) * 4,
        scratch_shapes=[
            pltpu.VMEM((2, blocks, rows + 2 * RIM, LANES), F32),
            pltpu.VMEM((8, 2, M, M), F32),
            pltpu.VMEM((8, 3, M, M), F32),
            pltpu.VMEM((slots + moved, M, M), F32),
            pltpu.VMEM((BATCH, 2, M, M), F32),
            pltpu.VMEM((BATCH, 2, M, M), F32),
            pltpu.VMEM((BATCH * M, 2 * M), BF16),
            pltpu.VMEM((BATCH * M, 2 * M), BF16),
            pltpu.VMEM((BATCH // 2, 2 * M, 2 * M), BF16),
            pltpu.VMEM((BATCH // 2, 2 * M, 2 * M), BF16),
            pltpu.SMEM((entries,), I32),
            pltpu.SMEM((entries,), I32),
            pltpu.SMEM((entries,), I32),
            pltpu.SemaphoreType.DMA((2,)),
        ],
        compiler_params=pltpu.CompilerParams(vmem_limit_bytes=40 << 20),
        name="patterns",
    )(
        owners, positions, counts, tags, measured, arrived.reshape(moved, M, M), object_field,
        sides, edges, corners, probe, *dft_tables(),
    )


def gather_kernel(
    sums_ref,
    left_ref,
    right_ref,
    probe_sums_ref,
    probe_ref,
    row_out,
    side_out,
    corner_out,
    probe_out,
    across,
    along,
    partial,
    send_sem,
    recv_sem,
):
    blocks = sums_ref.shape[1] - PADDED_BLOCKS
    rows = sums_ref.shape[2] - 2 * RIM
    n_ty, n_tx = lax.axis_size("ty"), lax.axis_size("tx")
    ty, tx = lax.axis_index("ty"), lax.axis_index("tx")
    strip = M // n_tx
    mine = pl.ds(pl.multiple_of(tx * strip, strip), strip)

    def at(down, right):
        return lax.rem(ty + down, n_ty), lax.rem(tx + right, n_tx)

    peers = [at(0, j) for j in range(1, n_tx)] + [at(j, 0) for j in range(1, n_ty)]
    peers += [neighbour(down, right) for down, right in CORNERS]
    barrier = pltpu.get_barrier_semaphore()
    for peer in peers:
        pl.semaphore_signal(barrier, inc=1, device_id=peer, device_id_type=MESH_ID)
    pl.semaphore_wait(barrier, len(peers))

    started = [0]

    def send(source, target, peer):
        slot = started[0]
        started[0] += 1
        copy = pltpu.make_async_remote_copy(
            src_ref=source,
            dst_ref=target,
            send_sem=send_sem.at[slot],
            recv_sem=recv_sem.at[slot],
            device_id=peer,
            device_id_type=MESH_ID,
        )
        copy.start()
        return copy

    first = []
    for j in range(1, n_tx):
        peer = at(0, j)
        there = pl.ds(pl.multiple_of(peer[1] * strip, strip), strip)
        first.append(send(probe_sums_ref.at[:, there, :], across.at[j], peer))
    main = rows + rows // 2
    corner = RIM + RIM // 2
    inner = pl.ds(1, blocks)
    rims = [
        send(right_ref.at[pl.ds(0, main)], side_out.at[0], neighbour(0, 1)),
        send(left_ref.at[pl.ds(0, main)], side_out.at[1], neighbour(0, -1)),
        send(sums_ref.at[:, inner, pl.ds(RIM + rows, RIM), :], row_out.at[0], neighbour(1, 0)),
        send(sums_ref.at[:, inner, pl.ds(0, RIM), :], row_out.at[1], neighbour(-1, 0)),
    ]
    for number, (down, right) in enumerate(CORNERS):
        packed = left_ref if right == -1 else right_ref
        start = main + (0 if down == -1 else corner)
        rims.append(send(packed.at[pl.ds(start, corner)], corner_out.at[number], neighbour(down, right)))

    total = probe_sums_ref[:, mine, :]
    for j in range(1, n_tx):
        first[j - 1].wait_recv()
        total = total + across[j]
    partial[...] = total
    second = [send(partial, along.at[j], at(j, 0)) for j in range(1, n_ty)]
    for j in range(1, n_ty):
        second[j - 1].wait_recv()
        total = total + along[j]
    weight = total[2] + tiny_level
    for part in range(2):
        probe_out[part, mine, :] = probe_ref[part, mine, :] - total[part] / weight
    third = [send(probe_out.at[:, mine, :], probe_out.at[:, mine, :], at(0, j)) for j in range(1, n_tx)]
    for copy in first + second:
        copy.wait_send()
    for copy in third + rims:
        copy.wait()


def gather(sums, left, right, probe_sums, probe, n_ty, n_tx):
    blocks = sums.shape[1] - PADDED_BLOCKS
    rows = sums.shape[2] - 2 * RIM
    main = rows + rows // 2
    strip = M // n_tx
    copies = 2 * (n_tx - 1) + (n_ty - 1) + 4 + len(CORNERS)
    return pl.pallas_call(
        gather_kernel,
        out_shape=(
            jax.ShapeDtypeStruct((2, 3, blocks, RIM, LANES), F32),
            jax.ShapeDtypeStruct((2, main, LANES), F32),
            jax.ShapeDtypeStruct((len(CORNERS), RIM + RIM // 2, LANES), F32),
            jax.ShapeDtypeStruct((2, M, M), F32),
        ),
        in_specs=[anywhere()] * 3 + [in_vmem()] * 2,
        out_specs=(anywhere(),) * 3 + (in_vmem(),),
        scratch_shapes=[
            pltpu.VMEM((n_tx, 3, strip, M), F32),
            pltpu.VMEM((n_ty, 3, strip, M), F32),
            pltpu.VMEM((3, strip, M), F32),
            pltpu.SemaphoreType.DMA((copies,)),
            pltpu.SemaphoreType.DMA((copies,)),
        ],
        compiler_params=pltpu.CompilerParams(
            collective_id=1, has_side_effects=True, vmem_limit_bytes=16 << 20
        ),
        name="gather",
    )(sums, left, right, probe_sums, probe)


def update_kernel(object_ref, sums_ref, row_ref, side_ref, corner_ref, probe_ref, object_out, probe_out):
    blocks = sums_ref.shape[1] - PADDED_BLOCKS
    chunk = object_ref.shape[1]
    step, steps = pl.program_id(0), pl.num_programs(0)
    rows = chunk * steps_of(side_ref, chunk)
    half = rows // 2
    at = pl.multiple_of(step * chunk, chunk)
    low = lane_ids(chunk) < RIM
    first_step, last_step = step == 0, step == steps - 1

    @pl.when(first_step)
    def _():
        probe_out[...] = probe_ref[...]

    def rolled(value):
        return pltpu.roll(value, RIM, 1)

    for block in range(blocks):
        totals = []
        for kind in range(3):
            value = sums_ref[kind, 1 + block]
            above = first_step & is_inside(-1, 0)
            below = last_step & is_inside(1, 0)
            value = value + jnp.where(above, row_ref[0, kind, block], 0.0)
            value = value + jnp.where(below, row_ref[1, kind, block], 0.0)
            if block in (0, blocks - 1):
                side = 0 if block == 0 else 1
                right = -1 if block == 0 else 1
                lanes = low if block == 0 else ~low
                if kind < 2:
                    rim = side_ref[side, pl.ds(at, chunk), :]
                    rim = rolled(rim) if kind else rim
                else:
                    late = at >= half
                    start = pl.multiple_of(rows + at - jnp.where(late, half, 0), chunk)
                    rim = side_ref[side, pl.ds(start, chunk), :]
                    rim = jnp.where(late, rolled(rim), rim)
                value = value + jnp.where(lanes & is_inside(0, right), rim, 0.0)
                for vertical, here in ((-1, first_step), (1, last_step)):
                    number = CORNERS.index((-vertical, -right))
                    if kind < 2:
                        rim = corner_ref[number, :RIM, :]
                        rim = rolled(rim) if kind else rim
                    else:
                        rim = corner_ref[number, RIM:, :]
                        rim = jnp.concatenate([rim, rolled(rim)], axis=0)
                    value = value + jnp.where(lanes & (here & is_inside(vertical, right)), rim, 0.0)
            totals.append(value)
        lit = totals[2] + floor_level
        at_lanes = slice(block * LANES, (block + 1) * LANES)
        for part in range(2):
            object_out[part, :, at_lanes] = object_ref[part, :, at_lanes] - totals[part] / lit


def steps_of(side_ref, chunk):
    return side_ref.shape[1] * 2 // 3 // chunk


def update(object_field, sums, edges, sides, corners, probe):
    rows, cols = object_field.shape[1:]
    chunk = RIM
    whole = lambda array: pl.BlockSpec(array.shape, lambda i: (0,) * array.ndim, memory_space=pltpu.VMEM)
    return pl.pallas_call(
        update_kernel,
        grid=(rows // chunk,),
        out_shape=(
            jax.ShapeDtypeStruct(object_field.shape, F32),
            jax.ShapeDtypeStruct(probe.shape, F32),
        ),
        in_specs=[
            pl.BlockSpec((2, chunk, cols), lambda i: (0, i, 0)),
            pl.BlockSpec((3, sums.shape[1], chunk, LANES), lambda i: (0, 0, i + 1, 0)),
            whole(edges),
            whole(sides),
            whole(corners),
            whole(probe),
        ],
        out_specs=(pl.BlockSpec((2, chunk, cols), lambda i: (0, i, 0)), whole(probe)),
        compiler_params=pltpu.CompilerParams(vmem_limit_bytes=24 << 20),
        name="update",
    )(object_field, sums, edges, sides, corners, probe)


def solution(mesh):
    n_ty, n_tx = mesh.shape["ty"], mesh.shape["tx"]

    def shards(measured, positions, owners, counts, object_field, probe_field):
        own = measured[0, 0]
        arrived, tags, sides, edges, corners = spread(owners, positions, counts, own, object_field)
        sums, left, right, probe_sums = patterns(
            owners, positions, counts, tags, own, arrived, object_field, sides, edges, corners, probe_field
        )
        edge_sums, side_sums, corner_sums, new_probe = gather(
            sums, left, right, probe_sums, probe_field, n_ty, n_tx
        )
        return update(object_field, sums, edge_sums, side_sums, corner_sums, new_probe)

    placed = (
        P("ty", "tx", None, None, None),
        P("ty", "tx", None, None),
        P("ty", "tx", None),
        P("ty", "tx"),
        P(None, "ty", "tx"),
        P(),
    )
    return jax.shard_map(
        shards, mesh=mesh, in_specs=placed, out_specs=(P(None, "ty", "tx"), P()), check_vma=False
    )
```

time: 1050 us -> 94.1 us (0.09); the launches traced: 1040 us -> 94.6 us
  waiting for transfers between devices: 421 us -> 0 us
  local copies, waits for them, and re-layouts: 270 us -> 9.12 us
  loops' own time: 101 us -> 0 us
  starting transfers between devices: 101 us -> 0 us
  Pallas kernels: 0 us -> 84.1 us
  other arithmetic: 73.1 us -> 0 us
  matrix products: 56.2 us -> 0 us
  between operations: 16.2 us -> 1.34 us
    psum x1 -> x0, waiting for transfers between devices: 256 us -> none  [shards(): summed = lax.psum((grad_real, grad_imag, weight), ('ty', 'tx'))]
    ppermute x32 -> x0, waiting for transfers between devices: 165 us -> none  [the longest x28 158 us: from_behind(): return lax.ppermute(block, axis, route)]
    another operation x7 -> x0, loops' own time: 101 us -> none  [the longest x3 100 us: add_patches(): return lax.fori_loop(0, spread.shape[0], add_one, accumulated)]
    ppermute x32 -> x0, starting transfers between devices: 101 us -> none  [the longest x28 92.5 us: from_behind(): return lax.ppermute(block, axis, route)]
    gather x105 -> x0, local copies, waits for them, and re-layouts: 99.3 us -> none
    dynamic_update_slice x24 -> x0, local copies, waits for them, and re-layouts: 96.8 us -> none  [add_one(): lax.dynamic_update_slice(current, window + spread[patch_id], (zero_index,...]
    pallas_call x0 -> x4, Pallas kernels: none -> 84.1 us  [the longest x1 35.2 us: gather(): pl.pallas_call(gather_kernel, out_shape=(jax.ShapeDtypeStruct((2, 3, bloc...]
    dot_general x48 -> x0, matrix products: 56.2 us -> none  [the longest x6 7.77 us: transform(): jnp.einsum('bjk,kl->bjl', left_imag, sine_table, precision=highest)]
  transfers between devices with their start and end apart: 33 -> 0, of which waited for: 10 -> 0; matrix products, arithmetic and copies ran while one was open for 6% -> 0% of each run, Pallas kernels for 0% -> 0%
where the time goes in v1:
time: 94.1 us; the launch traced here: 94.6 us
  Pallas kernels  84.1 us (89%)
  local copies, waits for them, and re-layouts  9.12 us (10%)
  between operations  1.34 us (1%)
    pallas_call x1, Pallas kernels, gather(): pl.pallas_call(gather_kernel, out_shape=(jax.ShapeDtypeStruct((2, 3, bloc...  35.2 us
    pallas_call x1, Pallas kernels, spread(): pl.pallas_call(spread_kernel, out_shape=(jax.ShapeDtypeStruct((ways, MOVE...  26.5 us
    pallas_call x1, Pallas kernels, patterns(): pl.pallas_call(patterns_kernel, out_shape=(jax.ShapeDtypeStruct((3, block...  18.2 us
    unnamed x23, local copies, waits for them, and re-layouts  9.12 us
    pallas_call x1, Pallas kernels, update(): pl.pallas_call(update_kernel, grid=(rows // chunk,), out_shape=(jax.Shape...  4.25 us

profile of v1, /device:TPU:1, one launch (start us, length us, event | category | flops | bytes accessed | tf_op | source)
XLA Modules:
  0.0 94.6 jit_solution(14399212374232105581)
XLA Ops:
  1.3 0.8 copy.13.positions_ref
  2.0 0.0 copy-start
  2.0 1.6 %copy-done = f32[2,512,512]{2,1,0:T(8,128)S(1)} copy-done((f32[2,512,512]{2,1,0:T(8,128)S(1)}, f32[2,512,512]{2,1,0:T(8,128)}, u32[]{:S(2)}) %copy-start) | copy-done | bytes 2097176
  3.6 0.0 copy-start.2
  3.6 1.6 %copy-done.2 = f32[1,1,32,128,128]{4,3,2,1,0:T(8,128)S(1)} copy-done((f32[1,1,32,128,128]{4,3,2,1,0:T(8,128)S(1)}, f32[1,1,32,128,128]{4,3,2,1,0:T(8,128)}, u32[]{:S(2)}) %copy-start.2) | copy-done | bytes 2097176
  5.2 0.0 copy-start.9
  5.2 0.7 copy-done.9
  5.9 0.0 copy-start.1
  5.9 0.0 copy-start.3
  5.9 0.0 copy-start.10
  5.9 26.5 %spread.1 = (f32[8,2,128,128]{3,2,1,0:T(8,128)S(1)}, s32[8,1,128]{2,1,0:T(1,128)S(1)}, f32[2,512,128]{2,1,0:T(8,128)S(1)}, f32[2,2,64,512]{3,2,1,0:T(8,128)S(1)}, f32[4,64,128]{2,1,0:T(8,128)S(1)}) custom-call(s32[1,1,32]{2,1,0:T(1,128)S(1)} %copy-done.9, s32[1,1,32,2]{3,2,1,0:T(8,128)S(1)} %copy.13.positions_ref, s32[1,1]{1,0:T(1,128)S(6)} %copy.14.counts_ref, ...), custom_call_target="tpu_custom_call" | custom-call | tf_op jit(solution)/shard_map/spread/pallas_call | solution.py:159
  32.4 0.0 copy-done.1
  32.4 0.0 copy-done.3
  32.4 0.0 copy-done.10
  32.4 0.0 copy-start.4
  32.4 0.9 copy-done.4
  33.3 0.0 copy-start.5
  33.3 0.9 copy-done.5
  34.2 0.0 copy-start.6
  34.2 0.9 copy-done.6
  35.1 0.0 copy-start.7
  35.1 0.9 copy-done.7
  36.0 0.0 copy-start.8
  36.0 0.9 copy-done.8
  36.9 18.2 %patterns.1 = (f32[3,6,640,128]{3,2,1,0:T(8,128)S(1)}, f32[960,128]{1,0:T(8,128)S(1)}, f32[960,128]{1,0:T(8,128)S(1)}, f32[3,128,128]{2,1,0:T(8,128)S(1)}) custom-call(s32[1,1,32]{2,1,0:T(1,128)S(1)} %copy-done.10, s32[1,1,32,2]{3,2,1,0:T(8,128)S(1)} %copy.13.positions_ref, s32[1,1]{1,0:T(1,128)S(6)} %copy.14.counts_ref, ...), custom_call_target="tpu_custom_call" | custom-call | tf_op jit(solution)/shard_map/patterns/pallas_call | solution.py:411
  55.2 35.2 %gather.1 = (f32[2,3,4,64,128]{4,3,2,1,0:T(8,128)S(1)}, f32[2,768,128]{2,1,0:T(8,128)S(1)}, f32[4,96,128]{2,1,0:T(8,128)S(1)}, f32[2,128,128]{2,1,0:T(8,128)S(1)}) custom-call(f32[3,6,640,128]{3,2,1,0:T(8,128)S(1)} %get-tuple-element.20.sums_ref, f32[960,128]{1,0:T(8,128)S(1)} %get-tuple-element.21.left_ref, f32[960,128]{1,0:T(8,128)S(1)} %get-tuple-element.22.right_ref, ...), custom_call_target="tpu_custom_call" | custom-call | tf_op jit(solution)/shard_map/gather/pallas_call | solution.py:538
  90.3 4.3 %update.1 = (f32[2,512,512]{2,1,0:T(8,128)}, f32[2,128,128]{2,1,0:T(8,128)}) custom-call(f32[2,512,512]{2,1,0:T(8,128)S(1)} %copy-done.1, f32[3,6,640,128]{3,2,1,0:T(8,128)S(1)} %get-tuple-element.20.sums_ref, f32[2,3,4,64,128]{4,3,2,1,0:T(8,128)S(1)} %get-tuple-element.24.row_ref, f32[2,768,128]{2,1,0:T(8,128)S(1)} %get-tuple-element.25.side_ref, ...), custom_call_target="tpu_custom_call" | custom-call | tf_op jit(solution)/shard_map/update/pallas_call | solution.py:624
Async XLA Ops:
  2.0 1.6 %copy-start = (f32[2,512,512]{2,1,0:T(8,128)S(1)}, f32[2,512,512]{2,1,0:T(8,128)}, u32[]{:S(2)}) copy-start(f32[2,512,512]{2,1,0:T(8,128)} %object_ref.5) | copy-start | bytes 6291460
  3.6 1.6 %copy-start.2 = (f32[1,1,32,128,128]{4,3,2,1,0:T(8,128)S(1)}, f32[1,1,32,128,128]{4,3,2,1,0:T(8,128)}, u32[]{:S(2)}) copy-start(f32[1,1,32,128,128]{4,3,2,1,0:T(8,128)} %param.10) | copy-start | bytes 6291460
  5.2 0.7 copy-start.9
  5.9 26.5 %copy-start.1 = (f32[2,512,512]{2,1,0:T(8,128)S(1)}, f32[2,512,512]{2,1,0:T(8,128)}, u32[]{:S(2)}) copy-start(f32[2,512,512]{2,1,0:T(8,128)} %object_ref.5) | copy-start | bytes 6291460
  5.9 26.5 %copy-start.3 = (f32[1,1,32,128,128]{4,3,2,1,0:T(8,128)S(1)}, f32[1,1,32,128,128]{4,3,2,1,0:T(8,128)}, u32[]{:S(2)}) copy-start(f32[1,1,32,128,128]{4,3,2,1,0:T(8,128)} %param.10) | copy-start | bytes 6291460
  5.9 26.5 %copy-start.10 = (s32[1,1,32]{2,1,0:T(1,128)S(1)}, s32[1,1,32]{2,1,0:T(1,128)}, u32[]{:S(2)}) copy-start(s32[1,1,32]{2,1,0:T(1,128)} %owners_ref.3) | copy-start | bytes 388
  32.4 0.9 copy-start.4
  33.3 0.9 copy-start.5
  34.2 0.9 copy-start.6
  35.1 0.9 copy-start.7
  36.0 0.9 copy-start.8

commit v2 on v1

v2 whole, which is shorter than its diff:
```python
import functools

import jax
import jax.numpy as jnp
import numpy as np
from jax import lax
from jax.experimental import pallas as pl
from jax.experimental.pallas import tpu as pltpu
from jax.sharding import PartitionSpec as P

M = 128
MOVE = 2
RIM = M // 2
LANES = 128
PADDED_BLOCKS = 2
SPARE_BLOCKS = 2
BATCH = 4

offset_level = 1.0
floor_level = 1.0
tiny_level = 1e-06

MESH_ID = pl.DeviceIdType.MESH
DIRECTIONS = [(-1, -1), (-1, 0), (-1, 1), (0, -1), (0, 1), (1, -1), (1, 0), (1, 1)]
CORNERS = [(-1, -1), (-1, 1), (1, -1), (1, 1)]

F32 = jnp.float32
BF16 = jnp.bfloat16
I32 = jnp.int32


def in_vmem():
    return pl.BlockSpec(memory_space=pltpu.VMEM)


def in_smem():
    return pl.BlockSpec(memory_space=pltpu.SMEM)


def dft_tables():
    phase = (np.outer(np.arange(M), np.arange(M)) % M) * (2.0 * np.pi / M)
    c, s = np.cos(phase) / np.sqrt(M), -np.sin(phase) / np.sqrt(M)
    forward = np.block([[c, s], [-s, c]])
    tables = []
    for table in (forward, forward.T):
        high = table.astype(BF16)
        tables += [high, (table - high.astype(np.float64)).astype(BF16)]
    return np.stack(tables)


def lane_ids(rows):
    return lax.broadcasted_iota(I32, (rows, LANES), 1)


def neighbour(down, right):
    ty, tx = lax.axis_index("ty"), lax.axis_index("tx")
    n_ty, n_tx = lax.axis_size("ty"), lax.axis_size("tx")
    return lax.rem(ty + (down + n_ty), n_ty), lax.rem(tx + (right + n_tx), n_tx)


def is_inside(down, right):
    ty, tx = lax.axis_index("ty"), lax.axis_index("tx")
    row, col = ty + down, tx + right
    return (row >= 0) & (row < lax.axis_size("ty")) & (col >= 0) & (col < lax.axis_size("tx"))


def pack_left(first, second, rows):
    return jnp.where(lane_ids(rows) >= RIM, first, pltpu.roll(second, RIM, 1))


def pack_right(first, second, rows):
    return jnp.where(lane_ids(rows) < RIM, first, pltpu.roll(second, RIM, 1))


def in_hbm():
    return pl.BlockSpec(memory_space=pltpu.HBM)


def kept_in_hbm(array):
    return pltpu.with_memory_space_constraint(array, pltpu.HBM)


def spread_kernel(
    owners_ref,
    positions_ref,
    counts_ref,
    measured_ref,
    object_ref,
    probe_ref,
    tables_ref,
    field,
    data,
    tag_out,
    shifted,
    tables,
    sums,
    arrived,
    sides,
    corners,
    probe,
    pattern_pack,
    tag_pack,
    side_pack,
    local_sem,
    send_sem,
    recv_sem,
):
    slots = measured_ref.shape[0]
    rows, cols = object_ref.shape[1:]
    blocks = cols // LANES
    n_tx = lax.axis_size("tx")
    ty, tx = lax.axis_index("ty"), lax.axis_index("tx")

    barrier = pltpu.get_barrier_semaphore()
    for down, right in DIRECTIONS:
        pl.semaphore_signal(barrier, inc=1, device_id=neighbour(down, right), device_id_type=MESH_ID)

    local = []

    def fetch(source, target):
        copy = pltpu.make_async_copy(source, target, local_sem.at[len(local)])
        copy.start()
        local.append(copy)
        return copy

    inner_rows = pl.ds(RIM, rows)
    edge_blocks = [0, blocks - 1]
    own_blocks = []
    for group in (edge_blocks, range(1, blocks - 1)):
        for block in group:
            own_blocks.append(
                fetch(object_ref.at[:, :, pl.ds(block * LANES, LANES)], field.at[:, 1 + block, inner_rows, :])
            )
    own_data = fetch(measured_ref, data.at[pl.ds(0, slots)])
    own_probe = fetch(probe_ref, probe)
    own_tables = fetch(tables_ref, tables)

    for copy in own_blocks[:2]:
        copy.wait()
    last = (blocks, inner_rows, slice(None))
    side_pack[0] = pack_left(field[(0,) + last], field[(1,) + last], rows)
    side_pack[1] = pack_right(field[0, 1, inner_rows, :], field[1, 1, inner_rows, :], rows)
    pl.semaphore_wait(barrier, len(DIRECTIONS))

    started = [0]

    def send(source, target, down, right):
        slot = started[0]
        started[0] += 1
        copy = pltpu.make_async_remote_copy(
            src_ref=source,
            dst_ref=target,
            send_sem=send_sem.at[slot],
            recv_sem=recv_sem.at[slot],
            device_id=neighbour(down, right),
            device_id_type=MESH_ID,
        )
        copy.start()
        return copy

    rims = [send(side_pack.at[0], sides.at[0], 0, 1), send(side_pack.at[1], sides.at[1], 0, -1)]
    for corner, (down, right) in enumerate(CORNERS):
        source = side_pack.at[0 if right == 1 else 1, pl.ds(0 if down == -1 else rows - RIM, RIM), :]
        rims.append(send(source, corners.at[corner], down, right))
    for copy in own_blocks[2:]:
        copy.wait()
    inner = pl.ds(1, blocks)
    lines = [
        send(field.at[:, inner, pl.ds(rows, RIM), :], field.at[:, inner, pl.ds(0, RIM), :], 1, 0),
        send(field.at[:, inner, pl.ds(RIM, RIM), :], field.at[:, inner, pl.ds(RIM + rows, RIM), :], -1, 0),
    ]

    own_data.wait()
    count = counts_ref[0, 0]
    lane = lane_ids(1)
    moves = []
    for way, (down, right) in enumerate(DIRECTIONS):
        target = jnp.where(is_inside(down, right), (ty + down) * n_tx + (tx + right), -1)
        found, first, second = jnp.int32(0), jnp.int32(0), jnp.int32(0)
        for slot in range(slots):
            hit = (owners_ref[0, 0, slot] == target) & (slot < count)
            first = jnp.where(hit & (found == 0), slot, first)
            second = jnp.where(hit & (found == 1), slot, second)
            found = found + hit.astype(I32)
        tag = jnp.zeros((1, LANES), I32)
        for index, chosen in enumerate((first, second)):
            pattern_pack[way, index] = data[chosen]
            valid = (found > index).astype(I32)
            tag = jnp.where(lane == 3 * index, valid, tag)
            tag = jnp.where(lane == 3 * index + 1, positions_ref[0, chosen], tag)
            tag = jnp.where(lane == 3 * index + 2, positions_ref[1, chosen], tag)
        tag_pack[way] = tag
    for way, (down, right) in enumerate(DIRECTIONS):
        moves.append(send(tag_pack.at[way], tag_out.at[way], down, right))
        moves.append(send(pattern_pack.at[way], arrived.at[pl.ds(way * MOVE, MOVE)], down, right))

    sums[...] = jnp.zeros(sums.shape, F32)
    spare = pl.ds(blocks + PADDED_BLOCKS, SPARE_BLOCKS)
    field[:, spare, pl.ds(0, M + 8), :] = jnp.zeros((2, SPARE_BLOCKS, M + 8, LANES), F32)
    own_probe.wait()
    for turn in range(8):
        for part in range(2):
            value = probe[part]
            shifted[turn, part] = pltpu.roll(value, turn, 0) if turn else value

    def unpacked(part, value):
        return value if part == 0 else pltpu.roll(value, RIM, 1)

    for copy in rims[:2]:
        copy.wait_recv()
    for part in range(2):
        field[part, 0, inner_rows, :] = jnp.where(is_inside(0, -1), unpacked(part, sides[0]), 0.0)
        field[part, 1 + blocks, inner_rows, :] = jnp.where(is_inside(0, 1), unpacked(part, sides[1]), 0.0)
    for corner, (down, right) in enumerate(CORNERS):
        rims[2 + corner].wait_recv()
        here = pl.ds(0, RIM) if down == 1 else pl.ds(RIM + rows, RIM)
        for part in range(2):
            field[part, 0 if right == 1 else 1 + blocks, here, :] = jnp.where(
                is_inside(-down, -right), unpacked(part, corners[corner]), 0.0
            )
    for line, (down, here) in zip(lines, ((-1, pl.ds(0, RIM)), (1, pl.ds(RIM + rows, RIM)))):
        line.wait()

        @pl.when(jnp.logical_not(is_inside(down, 0)))
        def _():
            field[:, inner, here, :] = jnp.zeros((2, blocks, RIM, LANES), F32)

    for copy in moves:
        copy.wait_recv()
    data[pl.ds(slots, arrived.shape[0])] = arrived[...]
    for copy in rims + moves:
        copy.wait_send()
    own_tables.wait()


def spread(owners, positions, counts, measured, object_field, probe_field):
    slots = measured.shape[0]
    rows, cols = object_field.shape[1:]
    blocks = cols // LANES
    ways = len(DIRECTIONS)
    copies = 4 + len(CORNERS) + 2 * ways
    all_blocks = blocks + PADDED_BLOCKS + SPARE_BLOCKS
    return pl.pallas_call(
        spread_kernel,
        out_shape=(
            jax.ShapeDtypeStruct((2, all_blocks, rows + 2 * RIM, LANES), F32),
            jax.ShapeDtypeStruct((slots + ways * MOVE, M, M), F32),
            jax.ShapeDtypeStruct((ways, 1, LANES), I32),
            jax.ShapeDtypeStruct((8, 2, M, M), F32),
            jax.ShapeDtypeStruct((4, 2 * M, 2 * M), BF16),
            jax.ShapeDtypeStruct((3, all_blocks, rows + 2 * RIM, LANES), F32),
        ),
        in_specs=[in_smem()] * 3 + [in_hbm()] * 4,
        out_specs=(in_vmem(),) * 6,
        scratch_shapes=[
            pltpu.VMEM((ways * MOVE, M, M), F32),
            pltpu.VMEM((2, rows, LANES), F32),
            pltpu.VMEM((len(CORNERS), RIM, LANES), F32),
            pltpu.VMEM((2, M, M), F32),
            pltpu.VMEM((ways, MOVE, M, M), F32),
            pltpu.VMEM((ways, 1, LANES), I32),
            pltpu.VMEM((2, rows, LANES), F32),
            pltpu.SemaphoreType.DMA((blocks + 3,)),
            pltpu.SemaphoreType.DMA((copies,)),
            pltpu.SemaphoreType.DMA((copies,)),
        ],
        compiler_params=pltpu.CompilerParams(
            collective_id=0, has_side_effects=True, vmem_limit_bytes=12 << 20
        ),
        name="spread",
    )(owners, positions, counts, *(kept_in_hbm(x) for x in (measured, object_field, probe_field, dft_tables())))


def dot(a, b):
    return jnp.dot(a, b, preferred_element_type=F32)


def patterns_kernel(
    owners_ref,
    positions_ref,
    counts_ref,
    tag_ref,
    data,
    field,
    shifted,
    tables,
    _,
    sums_ref,
    left_ref,
    right_ref,
    probe_sums_ref,
    turned_sums,
    window,
    framed,
    operands,
    row_list,
    col_list,
    data_list,
):
    slots = owners_ref.shape[2]
    rows = sums_ref.shape[2] - 2 * RIM
    blocks = sums_ref.shape[1] - PADDED_BLOCKS - SPARE_BLOCKS
    n_tx = lax.axis_size("tx")
    ty, tx = lax.axis_index("ty"), lax.axis_index("tx")
    self_index = ty * n_tx + tx
    forward, backward = (tables.at[0], tables.at[1]), (tables.at[2], tables.at[3])

    turned_sums[...] = jnp.zeros(turned_sums.shape, F32)

    count = counts_ref[0, 0]

    def own(slot, total):
        row_list[total] = positions_ref[0, slot]
        col_list[total] = positions_ref[1, slot]
        data_list[total] = slot
        return total + ((owners_ref[0, 0, slot] == self_index) & (slot < count)).astype(I32)

    total = lax.fori_loop(0, slots, own, jnp.int32(0), unroll=4)
    for way in range(len(DIRECTIONS)):
        for index in range(MOVE):
            row_list[total] = tag_ref[way, 0, 3 * index + 1]
            col_list[total] = tag_ref[way, 0, 3 * index + 2]
            data_list[total] = slots + way * MOVE + index
            total = total + tag_ref[way, 0, 3 * index]
    for index in range(BATCH):
        row_list[total + index] = 0
        col_list[total + index] = (blocks + PADDED_BLOCKS) * LANES - RIM
        data_list[total + index] = 0

    lane_of_frame = lane_ids(M)
    lane_of_window = lane_ids(M + 8)
    row_of_tile = lax.broadcasted_iota(I32, (8, LANES), 0)

    def place(step, index):
        number = step * BATCH + index
        row, col = row_list[number], col_list[number] + RIM
        turn, lane = row & 7, col & (LANES - 1)
        return number, pl.multiple_of(row - turn, 8), lax.shift_right_logical(col, 7), turn, lane

    def put_split(stage, pair, at, value):
        operands[stage, 0, pair, at[0], at[1]] = value.astype(BF16)
        low = value - operands[stage, 0, pair, at[0], at[1]].astype(F32)
        operands[stage, 1, pair, at[0], at[1]] = low.astype(BF16)

    def square(row, col):
        return pl.ds(row * M, M), pl.ds(col * M, M)

    def load(step, pair):
        for half in range(2):
            index = 2 * pair + half
            _, row, block, turn, lane = place(step, index)
            later = lane_of_window >= lane
            kept = row_of_tile >= turn
            parts = []
            for part in range(2):
                here = field[part, block, pl.ds(row, M + 8), :]
                beside = field[part, block + 1, pl.ds(row, M + 8), :]
                value = jnp.where(later, here, beside)
                value = jnp.concatenate([jnp.where(kept, value[:8], value[M:]), value[8:M]], axis=0)
                window[index, part] = value
                parts.append(value)
            wr, wi = parts
            pr = pltpu.roll(shifted[turn, 0], lane, 1)
            pi = pltpu.roll(shifted[turn, 1], lane, 1)
            framed[index, 0] = pr
            framed[index, 1] = pi
            put_split(0, pair, square(half, 0), pr * wr - pi * wi)
            put_split(0, pair, square(half, 1), pr * wi + pi * wr)

    def right_product(stage, pair, table):
        high, low = table
        a, b = operands[stage, 0, pair], operands[stage, 1, pair]
        value = dot(a, high[...]) + dot(b, high[...]) + dot(a, low[...])
        for half in range(2):
            for part in range(2):
                piece = value[half * M : (half + 1) * M, part * M : (part + 1) * M]
                put_split(stage + 1, pair, square(part, half), piece)

    def left_product(stage, pair, table):
        high, low = table
        a, b = operands[stage, 0, pair], operands[stage, 1, pair]
        return dot(high[...], a) + dot(high[...], b) + dot(low[...], a)

    def first_right(step, pair):
        right_product(0, pair, forward)

    def first_left(step, pair):
        far = left_product(1, pair, backward)
        for half in range(2):
            fr = far[:M, half * M : (half + 1) * M]
            fi = far[M:, half * M : (half + 1) * M]
            measured = data[data_list[step * BATCH + 2 * pair + half]]
            ratio = 1.0 - measured / (fr * fr + fi * fi + offset_level)
            put_split(2, pair, square(half, 0), fr * ratio)
            put_split(2, pair, square(half, 1), fi * ratio)

    def second_right(step, pair):
        right_product(2, pair, backward)

    def second_left(step, pair):
        back = left_product(3, pair, forward)
        for half in range(2):
            index = 2 * pair + half
            _, row, block, turn, lane = place(step, index)
            cr = back[:M, half * M : (half + 1) * M]
            ci = back[M:, half * M : (half + 1) * M]
            wr, wi = window[index, 0], window[index, 1]
            pr, pi = framed[index, 0], framed[index, 1]
            back_lanes = (LANES - lane) & (LANES - 1)
            terms = (wr * cr + wi * ci, wr * ci - wi * cr, wr * wr + wi * wi)
            for kind, term in enumerate(terms):
                turned_sums[turn, kind] += pltpu.roll(term, back_lanes, 1)
            later = lane_of_frame >= lane
            kept = row_of_tile >= turn
            terms = (pr * cr + pi * ci, pr * ci - pi * cr, pr * pr + pi * pi)
            for kind, term in enumerate(terms):
                for beside in range(2):
                    piece = jnp.where(later, 0.0, term) if beside else jnp.where(later, term, 0.0)
                    top = piece[:8]
                    piece = jnp.concatenate(
                        [jnp.where(kept, top, 0.0), piece[8:], jnp.where(kept, 0.0, top)], axis=0
                    )
                    sums_ref[kind, block + beside, pl.ds(row, M + 8), :] += piece

    phases = (load, first_right, first_left, second_right, second_left)
    pairs = BATCH // 2

    def one_batch(step, carry):
        for turn in range(len(phases) + pairs - 1):
            for pair in range(pairs):
                if 0 <= turn - pair < len(phases):
                    phases[turn - pair](step, pair)
        return carry

    lax.fori_loop(0, lax.div(total + (BATCH - 1), BATCH), one_batch, 0)

    for kind in range(3):
        total_of_kind = turned_sums[0, kind]
        for turn in range(1, 8):
            total_of_kind = total_of_kind + pltpu.roll(turned_sums[turn, kind], M - turn, 0)
        probe_sums_ref[kind] = total_of_kind

    half = rows // 2
    for pack, out, block in ((pack_left, left_ref, 0), (pack_right, right_ref, 1 + blocks)):
        def rim(kind, start, length):
            return sums_ref[kind, block, start : start + length, :]

        out[:rows, :] = pack(rim(0, RIM, rows), rim(1, RIM, rows), rows)
        out[rows : rows + half, :] = pack(rim(2, RIM, half), rim(2, RIM + half, half), half)
        at = rows + half
        for start in (0, RIM + rows):
            out[at : at + RIM, :] = pack(rim(0, start, RIM), rim(1, start, RIM), RIM)
            out[at + RIM : at + RIM + RIM // 2, :] = pack(
                rim(2, start, RIM // 2), rim(2, start + RIM // 2, RIM // 2), RIM // 2
            )
            at += RIM + RIM // 2


def patterns(owners, positions, counts, tags, data, field, shifted, tables, sums):
    rows = sums.shape[2] - 2 * RIM
    packed = rows + rows // 2 + 3 * RIM
    entries = data.shape[0] + BATCH
    return pl.pallas_call(
        patterns_kernel,
        out_shape=(
            jax.ShapeDtypeStruct(sums.shape, F32),
            jax.ShapeDtypeStruct((packed, LANES), F32),
            jax.ShapeDtypeStruct((packed, LANES), F32),
            jax.ShapeDtypeStruct((3, M, M), F32),
        ),
        in_specs=[in_smem()] * 4 + [in_vmem()] * 5,
        out_specs=(in_vmem(),) * 4,
        scratch_shapes=[
            pltpu.VMEM((8, 3, M, M), F32),
            pltpu.VMEM((BATCH, 2, M, M), F32),
            pltpu.VMEM((BATCH, 2, M, M), F32),
            pltpu.VMEM((4, 2, BATCH // 2, 2 * M, 2 * M), BF16),
            pltpu.SMEM((entries,), I32),
            pltpu.SMEM((entries,), I32),
            pltpu.SMEM((entries,), I32),
        ],
        input_output_aliases={8: 0},
        compiler_params=pltpu.CompilerParams(vmem_limit_bytes=16 << 20),
        name="patterns",
    )(owners, positions, counts, tags, data, field, shifted, tables, sums)


def gather_kernel(
    sums_ref,
    left_ref,
    right_ref,
    probe_sums_ref,
    probe_ref,
    field_ref,
    object_out,
    probe_out,
    lines,
    sides,
    corners,
    across,
    along,
    partial,
    send_sem,
    recv_sem,
):
    blocks = sums_ref.shape[1] - PADDED_BLOCKS - SPARE_BLOCKS
    rows = sums_ref.shape[2] - 2 * RIM
    half = rows // 2
    n_ty, n_tx = lax.axis_size("ty"), lax.axis_size("tx")
    ty, tx = lax.axis_index("ty"), lax.axis_index("tx")
    strip = M // n_tx
    mine = pl.ds(pl.multiple_of(tx * strip, strip), strip)

    def at(down, right):
        return lax.rem(ty + down, n_ty), lax.rem(tx + right, n_tx)

    peers = [at(0, j) for j in range(1, n_tx)] + [at(j, 0) for j in range(1, n_ty)]
    peers += [neighbour(down, right) for down, right in CORNERS]
    barrier = pltpu.get_barrier_semaphore()
    for peer in peers:
        pl.semaphore_signal(barrier, inc=1, device_id=peer, device_id_type=MESH_ID)
    pl.semaphore_wait(barrier, len(peers))

    started = [0]

    def send(source, target, peer):
        slot = started[0]
        started[0] += 1
        copy = pltpu.make_async_remote_copy(
            src_ref=source,
            dst_ref=target,
            send_sem=send_sem.at[slot],
            recv_sem=recv_sem.at[slot],
            device_id=peer,
            device_id_type=MESH_ID,
        )
        copy.start()
        return copy

    first = []
    for j in range(1, n_tx):
        peer = at(0, j)
        there = pl.ds(pl.multiple_of(peer[1] * strip, strip), strip)
        first.append(send(probe_sums_ref.at[:, there, :], across.at[j], peer))
    main = rows + half
    corner = RIM + RIM // 2
    inner = pl.ds(1, blocks)
    rims = [
        send(right_ref.at[pl.ds(0, main)], sides.at[0], neighbour(0, 1)),
        send(left_ref.at[pl.ds(0, main)], sides.at[1], neighbour(0, -1)),
        send(sums_ref.at[:, inner, pl.ds(RIM + rows, RIM), :], lines.at[0], neighbour(1, 0)),
        send(sums_ref.at[:, inner, pl.ds(0, RIM), :], lines.at[1], neighbour(-1, 0)),
    ]
    for number, (down, right) in enumerate(CORNERS):
        packed = left_ref if right == -1 else right_ref
        start = main + (0 if down == -1 else corner)
        rims.append(send(packed.at[pl.ds(start, corner)], corners.at[number], neighbour(down, right)))

    def rolled(value):
        return pltpu.roll(value, RIM, 1)

    def finish(block, start, length, totals):
        here = pl.ds(start, length)
        lit = 1.0 / (totals[2] + floor_level)
        for part in range(2):
            old = field_ref[part, 1 + block, pl.ds(start + RIM, length), :]
            object_out[part, here, block * LANES : (block + 1) * LANES] = old - totals[part] * lit

    def own(block, start, length):
        return [sums_ref[kind, 1 + block, pl.ds(start + RIM, length), :] for kind in range(3)]

    def side(block, start, length, late):
        index, right = (0, -1) if block == 0 else (1, 1)
        low = lane_ids(length) < RIM
        lanes = (low if block == 0 else jnp.logical_not(low)) & is_inside(0, right)
        there = sides[index, pl.ds(start, length), :]
        light = sides[index, pl.ds(start + (rows - half if late else rows), length), :]
        values = (there, rolled(there), rolled(light) if late else light)
        return [jnp.where(lanes, value, 0.0) for value in values]

    def plus(a, b):
        return [x + y for x, y in zip(a, b)]

    chunk = RIM

    def middle(step, carry):
        start = pl.multiple_of(step * chunk, chunk)
        for block in range(1, blocks - 1):
            finish(block, start, chunk, own(block, start, chunk))
        return carry

    lax.fori_loop(1, rows // chunk - 1, middle, 0)

    total = probe_sums_ref[:, mine, :]
    for j in range(1, n_tx):
        first[j - 1].wait_recv()
        total = total + across[j]
    partial[...] = total
    second = [send(partial, along.at[j], at(j, 0)) for j in range(1, n_ty)]
    for j in range(1, n_ty):
        second[j - 1].wait_recv()
        total = total + along[j]
    weight = total[2] + tiny_level
    for part in range(2):
        probe_out[part, mine, :] = probe_ref[part, mine, :] - total[part] / weight
    third = [send(probe_out.at[:, mine, :], probe_out.at[:, mine, :], at(0, j)) for j in range(1, n_tx)]

    for copy in rims:
        copy.wait_recv()
    for late in (False, True):

        def outer(step, carry):
            start = pl.multiple_of(step * chunk, chunk)
            for block in (0, blocks - 1):
                finish(block, start, chunk, plus(own(block, start, chunk), side(block, start, chunk, late)))
            return carry

        middle_step = half // chunk
        lax.fori_loop(*((middle_step, rows // chunk - 1) if late else (1, middle_step)), outer, 0)
    for line, down in enumerate((-1, 1)):
        start = 0 if down == -1 else rows - RIM
        for block in range(blocks):
            totals = own(block, start, RIM)
            arrived = [jnp.where(is_inside(down, 0), lines[line, kind, block], 0.0) for kind in range(3)]
            totals = plus(totals, arrived)
            if block in (0, blocks - 1):
                totals = plus(totals, side(block, start, RIM, down == 1))
                right = -1 if block == 0 else 1
                number = CORNERS.index((-down, -right))
                low = lane_ids(RIM) < RIM
                lanes = (low if block == 0 else jnp.logical_not(low)) & is_inside(down, right)
                there = corners[number, :RIM, :]
                light = corners[number, RIM:, :]
                values = (there, rolled(there), jnp.concatenate([light, rolled(light)], axis=0))
                totals = plus(totals, [jnp.where(lanes, value, 0.0) for value in values])
            finish(block, start, RIM, totals)

    for copy in first + second + rims:
        copy.wait_send()
    for copy in third:
        copy.wait()


def gather(sums, left, right, probe_sums, probe, field, n_ty, n_tx):
    blocks = sums.shape[1] - PADDED_BLOCKS - SPARE_BLOCKS
    rows = sums.shape[2] - 2 * RIM
    main = rows + rows // 2
    strip = M // n_tx
    copies = 2 * (n_tx - 1) + (n_ty - 1) + 4 + len(CORNERS)
    return pl.pallas_call(
        gather_kernel,
        out_shape=(
            jax.ShapeDtypeStruct((2, rows, blocks * LANES), F32),
            jax.ShapeDtypeStruct((2, M, M), F32),
        ),
        in_specs=[in_vmem()] * 6,
        out_specs=(in_vmem(),) * 2,
        scratch_shapes=[
            pltpu.VMEM((2, 3, blocks, RIM, LANES), F32),
            pltpu.VMEM((2, main, LANES), F32),
            pltpu.VMEM((len(CORNERS), RIM + RIM // 2, LANES), F32),
            pltpu.VMEM((n_tx, 3, strip, M), F32),
            pltpu.VMEM((n_ty, 3, strip, M), F32),
            pltpu.VMEM((3, strip, M), F32),
            pltpu.SemaphoreType.DMA((copies,)),
            pltpu.SemaphoreType.DMA((copies,)),
        ],
        compiler_params=pltpu.CompilerParams(
            collective_id=1, has_side_effects=True, vmem_limit_bytes=12 << 20
        ),
        name="gather",
    )(sums, left, right, probe_sums, probe, field)


def solution(mesh):
    n_ty, n_tx = mesh.shape["ty"], mesh.shape["tx"]

    def shards(measured, positions, owners, counts, object_field, probe_field):
        positions, owners = kept_in_hbm(positions[0, 0].T), kept_in_hbm(owners)
        field, data, tags, shifted, tables, sums = spread(
            owners, positions, counts, measured[0, 0], object_field, probe_field
        )
        sums, left, right, probe_sums = patterns(
            owners, positions, counts, tags, data, field, shifted, tables, sums
        )
        return gather(sums, left, right, probe_sums, probe_field, field, n_ty, n_tx)

    placed = (
        P("ty", "tx", None, None, None),
        P("ty", "tx", None, None),
        P("ty", "tx", None),
        P("ty", "tx"),
        P(None, "ty", "tx"),
        P(),
    )
    return jax.shard_map(
        shards, mesh=mesh, in_specs=placed, out_specs=(P(None, "ty", "tx"), P()), check_vma=False
    )
```

time: 94.1 us -> 77.5 us (0.82)
  Pallas kernels: 84.1 us -> 75.1 us
  local copies, waits for them, and re-layouts: 9.12 us -> 1.98 us
    pallas_call x4 -> x3, Pallas kernels: 84.1 us -> 75.1 us  [the longest x1 37.9 us: gather(): pl.pallas_call(gather_kernel, out_shape=(jax.ShapeDtypeStruct((2, rows, b...]
    unnamed x23 -> x4, local copies, waits for them, and re-layouts: 9.12 us -> 1.98 us
where the time goes in v2:
time: 77.5 us; the launch traced here: 78.4 us
  Pallas kernels  75.1 us (97%)
  local copies, waits for them, and re-layouts  1.98 us (3%)
  between operations  1.32 us (2%)
    pallas_call x1, Pallas kernels, gather(): pl.pallas_call(gather_kernel, out_shape=(jax.ShapeDtypeStruct((2, rows, b...  37.9 us
    pallas_call x1, Pallas kernels, spread(): pl.pallas_call(spread_kernel, out_shape=(jax.ShapeDtypeStruct((2, all_blo...  26.6 us
    pallas_call x1, Pallas kernels, patterns(): pl.pallas_call(patterns_kernel, out_shape=(jax.ShapeDtypeStruct(sums.shap...  10.6 us
    unnamed x4, local copies, waits for them, and re-layouts  1.98 us

profile of v2, /device:TPU:1, one launch (start us, length us, event | category | flops | bytes accessed | tf_op | source)
XLA Modules:
  0.0 78.4 jit_solution(5313945626856448860)
XLA Ops:
  1.3 26.6 %spread.1 = (f32[2,8,640,128]{3,2,1,0:T(8,128)S(1)}, f32[48,128,128]{2,1,0:T(8,128)S(1)}, s32[8,1,128]{2,1,0:T(1,128)S(1)}, f32[8,2,128,128]{3,2,1,0:T(8,128)S(1...) custom-call(s32[1,1,32]{2,1,0:T(1,128)} %owners_ref.3, s32[2,32]{1,0:T(2,128)} %bitcast.5, ...), custom_call_target="tpu_custom_call" | custom-call | tf_op jit(solution)/shard_map/spread/pallas_call | solution.py:243
  27.9 0.0 copy-start
  27.9 10.6 %patterns.1 = (f32[3,8,640,128]{3,2,1,0:T(8,128)S(1)}, f32[960,128]{1,0:T(8,128)S(1)}, f32[960,128]{1,0:T(8,128)S(1)}, f32[3,128,128]{2,1,0:T(8,128)S(1)}) custom-call(s32[1,1,32]{2,1,0:T(1,128)} %owners_ref.3, s32[2,32]{1,0:T(2,128)} %bitcast.6, s32[1,1]{1,0:T(1,128)S(6)} %copy.13.counts_ref, ...), custom_call_target="tpu_custom_call", output_to_operand_aliasing={{0}: (8, {})} | custom-call | tf_op jit(solution)/shard_map/patterns/pallas_call | solution.py:463
  38.5 0.0 copy-done
  38.5 37.9 %gather.1 = (f32[2,512,512]{2,1,0:T(8,128)S(1)}, f32[2,128,128]{2,1,0:T(8,128)S(1)}) custom-call(f32[3,8,640,128]{3,2,1,0:T(8,128)S(1)} %get-tuple-element.18.sums_ref, f32[960,128]{1,0:T(8,128)S(1)} %get-tuple-element.19.left_ref, f32[960,128]{1,0:T(8,128)S(1)} %get-tuple-element.20.right_ref, f32[3,128,128]{2,1,0:T(8,128)S(1)} %get-tuple-element.21.probe_sums_ref, ...), custom_call_target="tpu_custom_call" | custom-call | tf_op jit(solution)/shard_map/gather/pallas_call | solution.py:650
  76.4 1.3 %copy.14 = f32[2,512,512]{2,1,0:T(8,128)} copy(f32[2,512,512]{2,1,0:T(8,128)S(1)} %get-tuple-element.24) | data formatting | bytes 4194304
  77.8 0.7 copy.15
Async XLA Ops:
  27.9 10.6 %copy-start = (f32[2,128,128]{2,1,0:T(8,128)S(1)}, f32[2,128,128]{2,1,0:T(8,128)}, u32[]{:S(2)}) copy-start(f32[2,128,128]{2,1,0:T(8,128)} %probe_ref.3) | copy-start | bytes 393220
